TPU v7x, 128 devices: a whole 4x4x4 slice. The times are simulated.
128 devices in a mesh: row: 16 (over z_lo, x, core), col: 8 (over z_hi, y).
Axes of the slice: x: 4, y: 4, z: 4 (z_hi: 2, z_lo: 2; z = z_hi * 2 + z_lo), core: 2. Of those that a mesh axis runs over, the one named last changes fastest.
Arguments:
- density: bfloat16 [64, 5, 256, 256], P('row', None, 'col'), may hold values from -1 to 2, as said below
- pattern: int32 [64, 5], P('row'), may hold values from 0 to 1, as said below
- windows: int32 [256], P(('row', 'col')), may hold values from 0 to 125, as said below
- basis_values: bfloat16 [256, 4096, 384], P(('row', 'col')), may hold values from -6 to 6
- basis_grads: bfloat16 [3, 256, 4096, 384], P(None, ('row', 'col')), may hold values from -48 to 48
- weights: float32 [256, 4096], P(('row', 'col')), may hold values from 0.25 to 4
Outputs:
- purified: bfloat16 [64, 5, 256, 256], P('row', None, 'col')
- xc_matrix: float32 [64, 5, 256, 256], P('row', None, 'col')
- grid_density: float32 [256, 4096], P(('row', 'col'))
Inputs may be any that keep to these rules, and one draw needn't show every extreme that they name: density[i, d] is block (i, i + d - 2) of a symmetric matrix: density[i, d] equals density[i + d - 2, 4 - d] transposed; blocks whose column block lies outside the matrix are 0. pattern[i, d] = pattern[i + d - 2, 4 - d]; it is 1 for d = 1, 2, 3 where block i + d - 2 exists and 0 where it does not. Tile t lies on device t // 2 of the joined axes row+col; if that device has row index q, windows[t] lies between 2 * 4 q - 2 and 2 * 4 q + 2 * 4 - 1.
All inputs are finite; a program needn't handle non-finite values.
Results may differ from a plain program's by a relative error of at most 0.011.
Values may be sent and summed in bfloat16 or wider, within the bound.
A program may use at most 128 MiB of HBM per device.

v0:
```python
import jax
import jax.numpy as jnp
from jax import lax
from jax.sharding import Mesh
from jax.sharding import PartitionSpec as P

ITERS = 2
COL = ("col_0", "col_1")
ROW_COL = ("row", "col_0", "col_1")


slater_cx = 0.7386
kappa_pbe = 0.804
mu_pbe = 0.2195


def shifted_2(value, axis, by):
    length = lax.axis_size(axis)
    pairs = [(i, i + by) for i in range(length) if 0 <= i + by < length]
    return lax.ppermute(value, axis, pairs)


def padded(cells, sides, width):
    for axis, dim in sides:
        count = lax.axis_size(axis)
        ends = count - 1
        head = lax.slice_in_dim(cells, 0, width, axis=dim)
        tail = lax.slice_in_dim(cells, cells.shape[dim] - width, cells.shape[dim], axis=dim)
        cells = jnp.concatenate(
            [
                lax.ppermute(tail, axis, [(i, (i + 1) % count) for i in range(ends)]),
                cells,
                lax.ppermute(head, axis, [((i + 1) % count, i) for i in range(ends)]),
            ],
            axis=dim,
        )
    return cells


def in_order(pieces, dim):
    pieces = jnp.moveaxis(pieces, 0, dim)
    lengths = pieces.shape
    return pieces.reshape(*lengths[:dim], lengths[dim] * lengths[dim + 1], *lengths[dim + 2 :])


def sent_to_all(value, axis):
    length = lax.axis_size(axis)
    return lax.all_to_all(
        jnp.broadcast_to(value[None], (length, *value.shape)), axis, 0, 0, tiled=True
    )


def gather_directly(value, axis, dim):
    return in_order(sent_to_all(value, axis), dim)


def sum_in_order(pieces, axes, sequence):
    inside = pieces.shape[1:]
    pieces = pieces.reshape(*(lax.axis_size(a) for a in axes), *inside)
    pieces = jnp.moveaxis(pieces, sequence, range(len(axes))).reshape(-1, *inside)
    for k in sequence:
        pieces = lax.psum_scatter(pieces, axes[k], scatter_dimension=0, tiled=True)
    return pieces[0]


def cut_along(value, dim, length):
    before, after = (value.shape[:dim], value.shape[dim + 1 :])
    return jnp.moveaxis(value.reshape(*before, length, -1, *after), dim, 0)


def scatter_axes(value, axes, sequence, dim):
    length = lax.axis_size(axes)
    return sum_in_order(cut_along(value, dim, length), axes, sequence)


def energy_sum(point_density, grad_square):
    spread = jnp.sqrt(point_density * point_density + 1.0)
    reduced = grad_square / spread ** (8.0 / 3.0)
    enhance = 1.0 + kappa_pbe - kappa_pbe / (1.0 + mu_pbe * reduced / kappa_pbe)
    return jnp.sum(-slater_cx * spread ** (4.0 / 3.0) * enhance)


def tile_terms(values, grads, quadrature, window_block):
    functions = values.shape[1]
    points = values.shape[0]
    projected = jnp.dot(values, window_block, preferred_element_type=jnp.float32)
    point_density = jnp.sum(projected * values.astype(jnp.float32), axis=1) / functions
    slopes = 2.0 * jnp.sum(projected[None] * grads.astype(jnp.float32), axis=2) / functions
    grad_square = jnp.sum(slopes * slopes, axis=0)
    by_density, by_gradient = jax.grad(energy_sum, argnums=(0, 1))(point_density, grad_square)
    scaled = quadrature / points
    weighted = (0.5 * by_density * scaled)[:, None] * values.astype(jnp.float32)
    weighted = weighted + jnp.sum(
        ((2.0 * by_gradient * scaled)[None] * slopes)[:, :, None] * grads.astype(jnp.float32),
        axis=0,
    )
    weighted = weighted.astype(jnp.bfloat16)
    one_side = lax.dot_general(
        values, weighted, (((0,), (0,)), ((), ())), preferred_element_type=jnp.float32
    )
    return (point_density, one_side + one_side.T)


def band_product(left, right_padded):
    blocks = left.shape[0]
    total = None
    for offset_step in range(5):
        shifted = right_padded[offset_step : offset_step + blocks]
        widened = jnp.pad(shifted, ((0, 0), (2, 2), (0, 0), (0, 0)))
        picked = widened[:, 4 - offset_step : 9 - offset_step]
        term = jnp.einsum(
            "brk,bdkc->bdrc", left[:, offset_step], picked, preferred_element_type=jnp.float32
        )
        total = term if total is None else total + term
    return total


def window_of(band_three, lead, offset, functions):
    paired = lax.dynamic_slice_in_dim(band_three, lead, 2, 0)
    upper = jnp.concatenate([paired[0, 1], paired[0, 2]], axis=1)
    lower = jnp.concatenate([paired[1, 0], paired[1, 1]], axis=1)
    dense = jnp.concatenate([upper, lower], axis=0)
    return lax.dynamic_slice(dense, (offset, offset), (functions, functions))


def spread_term(summed, term, lead, offset):
    width = summed.shape[2]
    dense = lax.dynamic_update_slice(
        jnp.zeros((2 * width, 2 * width), summed.dtype), term, (offset, offset)
    )
    nothing = jnp.zeros((width, width), summed.dtype)
    upper = jnp.stack([nothing, dense[:width, :width], dense[:width, width:]])
    lower = jnp.stack([dense[width:, :width], dense[width:, width:], nothing])
    increment = jnp.stack([upper, lower])
    paired = lax.dynamic_slice_in_dim(summed, lead, 2, 0)
    return lax.dynamic_update_slice_in_dim(summed, paired + increment, lead, 0)


def edge_rows(summed):
    blocks = summed.shape[0] - 2
    from_above = shifted_2(summed[0].astype(jnp.bfloat16), "row", -1).astype(jnp.float32)
    from_below = shifted_2(summed[blocks + 1].astype(jnp.bfloat16), "row", 1).astype(jnp.float32)
    own_rows = summed[1 : blocks + 1]
    return jnp.concatenate(
        [
            own_rows[:1] + from_below[None],
            own_rows[1 : blocks - 1],
            own_rows[blocks - 1 :] + from_above[None],
        ],
        axis=0,
    )


def on_device(density, pattern, windows, basis_values, basis_grads, weights):
    row_index = lax.axis_index("row")
    band_rows = density.shape[0]
    functions = basis_values.shape[2]
    step_size = functions // 3
    kept = (pattern > 0)[:, :, None, None]
    current = jnp.where(kept, density, jnp.zeros_like(density))
    for iteration in range(ITERS):
        near_right = padded(current, (("row", 0),), 2)
        right_full = lax.all_gather(near_right, COL, axis=2, tiled=True)
        square = jnp.where(kept, band_product(current, right_full), 0.0).astype(jnp.bfloat16)
        cubic = band_product(square, right_full)
        current = jnp.where(kept, 3.0 * square.astype(jnp.float32) - 2.0 * cubic, 0.0).astype(
            jnp.bfloat16
        )
    rows_band = gather_directly(current[:, 1:4], COL, 2)
    near = padded(rows_band, (("row", 0),), 1)
    tiles_here = windows.shape[0]
    points = basis_values.shape[1]
    block_size = near.shape[2]

    def one_tile(tile_index, carry):
        summed, densities = carry
        position = tile_index.astype(jnp.int32)
        start_step = windows[position]
        lead = start_step // 2 - (band_rows * row_index - 1)
        offset = start_step % 2 * step_size
        window_block = window_of(near, lead, offset, functions)
        values = lax.dynamic_index_in_dim(basis_values, position, 0, keepdims=False)
        grads = lax.dynamic_index_in_dim(basis_grads, position, 1, keepdims=False)
        quadrature = lax.dynamic_index_in_dim(weights, position, 0, keepdims=False)
        point_density, contribution = tile_terms(values, grads, quadrature, window_block)
        summed = spread_term(summed, contribution, lead, offset)
        densities = lax.dynamic_update_index_in_dim(densities, point_density, position, 0)
        return (summed, densities)

    start_carry = (
        jnp.zeros((band_rows + 2, 3, block_size, block_size), jnp.float32),
        jnp.zeros((tiles_here, points), jnp.float32),
    )
    local_terms, densities = lax.fori_loop(0, tiles_here, one_tile, start_carry)
    owner_part = scatter_axes(local_terms.astype(jnp.bfloat16), COL, (1, 0), 2).astype(jnp.float32)
    mine = edge_rows(owner_part)
    xc_matrix = jnp.where(kept, jnp.pad(mine, ((0, 0), (1, 1), (0, 0), (0, 0))), 0.0)
    return (current, xc_matrix, densities)


def solution(mesh):
    torus = Mesh(mesh.devices.reshape(mesh.shape["row"], 2, 4), ("row", "col_0", "col_1"))
    placed = (
        P("row", None, COL, None),
        P("row", None),
        P(ROW_COL),
        P(ROW_COL, None, None),
        P(None, ROW_COL, None, None),
        P(ROW_COL, None),
    )
    return jax.shard_map(
        on_device,
        mesh=torus,
        in_specs=placed,
        out_specs=(P("row", None, COL, None), P("row", None, COL, None), P(ROW_COL, None)),
        check_vma=False,
    )
```

profile of v0, /device:TPU:1, one launch (start us, length us, event | category | flops | bytes accessed | tf_op | source)
XLA Modules:
  0.0 433.7 jit_solution(14375397627598703558)
XLA Ops:
  7.2 0.7 broadcast_compare_fusion
  8.0 1.1 copy_select_fusion
  9.1 4.5 %collective-permute-start = (bf16[2,5,32,256]{3,2,0,1:T(8,128)(2,1)S(1)}, bf16[2,5,32,256]{3,2,0,1:T(8,128)(2,1)S(1)}, u32[]{:S(2)}, u32[]{:S(2)}) collective-permute-start(bf16[2,5,32,256]{3,2,0,1:T(8,128)(2,1)S(1)} %get-tuple-element.389), channel_id=1, source_target_pairs={{0,8},{8,16},{16,24},{24,32},{32,40},{40,48},{48,56},{56,64},{64,7... | collective-permute-start | bytes 491528 | tf_op jit(solution)/shard_map/ppermute | solution.py:31
  13.6 1.9 collective-permute-start.1
  15.9 4.4 %collective-permute-done.1 = bf16[2,5,32,256]{3,2,0,1:T(8,128)(2,1)S(1)} collective-permute-done((bf16[2,5,32,256]{3,2,0,1:T(8,128)(2,1)S(1)}, bf16[2,5,32,256]{3,2,0,1:T(8,128)(2,1)S(1)}, u32[]{:S(2)}, u32[]{:S(2)}) %collective-permute-start.1) | collective-permute-done | bytes 163872 | tf_op jit(solution)/shard_map/ppermute | solution.py:33
  20.3 0.9 pad_maximum_fusion.1
  21.2 83.0 %all-gather.3.cloned.1.call-done = bf16[8,5,256,256]{3,2,0,1:T(8,128)(2,1)} async-done(((bf16[8,5,32,256]{3,2,0,1:T(8,128)(2,1)}), bf16[8,5,256,256]{3,2,0,1:T(8,128)(2,1)}) %all-gather.3.cloned.1.call-update) | async-done | bytes 5242896 | tf_op jit(solution)/shard_map/all_gather | solution.py:163
  104.3 4.5 %fusion.153 = (bf16[4,5,256,256]{3,2,0,1:T(8,128)(2,1)S(1)}, bf16[4,5,256,256]{3,2,0,1:T(8,128)(2,1)S(1)}, bf16[4,5,256,256]{3,2,0,1:T(8,128)(2,1)S(1)}, bf16[4,5,256,256]{3,2,0,1:T(8,128)(2,1)S(1)}) fusion(bf16[8,5,256,256]{3,2,0,1:T(8,128)(2,1)} %all-gather.3.cloned.1.call-done), kind=kLoop, calls=%fused_computation.165 | loop fusion | bytes 20971520 | tf_op jit(solution)/shard_map/slice | solution.py:108
  110.5 1.7 copy-done.1
  112.2 0.5 fusion.128
  114.5 0.6 fusion.113
  115.1 4.4 %collective-permute-start.2 = (bf16[2,5,32,256]{3,2,0,1:T(8,128)(2,1)S(1)}, bf16[2,5,32,256]{3,2,0,1:T(8,128)(2,1)S(1)}, u32[]{:S(2)}, u32[]{:S(2)}) collective-permute-start(bf16[2,5,32,256]{3,2,0,1:T(8,128)(2,1)S(1)} %get-tuple-element.387), channel_id=1, source_target_pairs={{0,8},{8,16},{16,24},{24,32},{32,40},{40,48},{48,56},{56,64},{64,7... | collective-permute-start | bytes 491528 | tf_op jit(solution)/shard_map/ppermute | solution.py:31
  119.5 1.9 collective-permute-start.3
  121.7 4.4 %collective-permute-done.3 = bf16[2,5,32,256]{3,2,0,1:T(8,128)(2,1)S(1)} collective-permute-done((bf16[2,5,32,256]{3,2,0,1:T(8,128)(2,1)S(1)}, bf16[2,5,32,256]{3,2,0,1:T(8,128)(2,1)S(1)}, u32[]{:S(2)}, u32[]{:S(2)}) %collective-permute-start.3) | collective-permute-done | bytes 163872 | tf_op jit(solution)/shard_map/ppermute | solution.py:33
  126.1 0.9 pad_maximum_fusion.2
  127.1 78.4 %all-gather.5.cloned.1.call-done = bf16[8,5,256,256]{3,2,0,1:T(8,128)(2,1)} async-done(((bf16[8,5,32,256]{3,2,0,1:T(8,128)(2,1)}), bf16[8,5,256,256]{3,2,0,1:T(8,128)(2,1)}) %all-gather.5.cloned.1.call-update) | async-done | bytes 5242896 | tf_op jit(solution)/shard_map/all_gather | solution.py:163
  205.5 4.5 %fusion.152 = (bf16[4,5,256,256]{3,2,0,1:T(8,128)(2,1)S(1)}, bf16[4,5,256,256]{3,2,0,1:T(8,128)(2,1)S(1)}, bf16[4,5,256,256]{3,2,0,1:T(8,128)(2,1)S(1)}, bf16[4,5,256,256]{3,2,0,1:T(8,128)(2,1)S(1)}) fusion(bf16[8,5,256,256]{3,2,0,1:T(8,128)(2,1)} %all-gather.5.cloned.1.call-done), kind=kLoop, calls=%fused_computation.164 | loop fusion | bytes 20971520 | tf_op jit(solution)/shard_map/slice | solution.py:108
  210.5 0.5 fusion.39
  211.7 1.7 copy-done.2
  213.4 0.5 fusion.125
  215.7 0.6 fusion.119
  216.5 24.1 %all_to_all.5 = bf16[8,4,3,32,256]{4,3,2,1,0:T(8,128)(2,1)S(1)} all-to-all(bf16[8,4,3,32,256]{4,3,2,1,0:T(8,128)(2,1)S(1)} %broadcast_in_dim.83), channel_id=1, replica_groups=mesh['row'=16,'col_0'=2,'col_1'=4] {'col_0','col_1'}, dimensions={0} | all-to-all | bytes 3145728 | tf_op jit(solution)/shard_map/all_to_all | solution.py:48
  240.9 5.1 %collective-permute-start.4 = (bf16[1,3,256,256]{3,2,1,0:T(8,128)(2,1)S(1)}, bf16[1,3,256,256]{3,2,1,0:T(8,128)(2,1)S(1)}, u32[]{:S(2)}, u32[]{:S(2)}) collective-permute-start(bf16[1,3,256,256]{3,2,1,0:T(8,128)(2,1)S(1)} %bitcast.239), channel_id=1, source_target_pairs={{0,8},{8,16},{16,24},{24,32},{32,40},{40,48},{48,56},{56,64},{64,7... | collective-permute-start | bytes 1179656 | tf_op jit(solution)/shard_map/ppermute | solution.py:31
  246.0 2.1 collective-permute-start.5
  248.1 2.6 collective-permute-done.4
  250.7 4.4 %collective-permute-done.5 = bf16[1,3,256,256]{3,2,1,0:T(8,128)(2,1)S(1)} collective-permute-done((bf16[1,3,256,256]{3,2,1,0:T(8,128)(2,1)S(1)}, bf16[1,3,256,256]{3,2,1,0:T(8,128)(2,1)S(1)}, u32[]{:S(2)}, u32[]{:S(2)}) %collective-permute-start.5) | collective-permute-done | bytes 393248 | tf_op jit(solution)/shard_map/ppermute | solution.py:33
  255.1 1.7 pad_maximum_fusion
  256.8 2.6 broadcast_in_dim.81
  259.4 99.6 %while.18 = (s32[]{:T(128)}, f32[6,3,256,256]{3,2,1,0:T(8,128)}, f32[2,4096]{1,0:T(2,128)}, s32[2]{0:T(128)}, s32[]{:T(128)}, /*index=5*/bf16[2,4096,384]{2,1,0:...) while((s32[]{:T(128)}, f32[6,3,256,256]{3,2,1,0:T(8,128)}, ...), condition=%wide.region_5.6_spmd, body=%wide.region_0.5_spmd.sunk | while | flops 2456809472 | bytes 116916952 | solution.py:194
  259.4 1.3 dynamic_slice.135
  263.3 0.7 dynamic-slice_bitcast_fusion.5
  264.0 2.2 constant_dynamic-slice_fusion.2
  266.2 3.0 copy.330
  269.2 7.4 %multiply_reduce_fusion.4 = (f32[4096]{0:T(1024)S(1)}, f32[4096,384]{0,1:T(8,128)}) fusion(bf16[1,4096,384]{1,2,0:T(8,128)(2,1)} %copy.330, s32[]{:T(128)S(6)} %select_n.130, bf16[256,256]{1,0:T(8,128)(2,1)} %get-tuple-element.462, bf16[256,256]{1,0:T(8,128)(2,1)S(1)} %get-tuple-element.463, bf16[256,256]{1,0:T(8,128)(2,1)S(1)} %get-tuple-element.464, ...), kind=kOutput, calls=%fused_computation.6.clone.1 | convolution fusion | flops 1213853696 | bytes 13123588 | tf_op jit(solution)/shard_map/while/body/eval_jaxpr/dot_general | solution.py:86
  276.6 6.6 %copy.331 = f32[4096,384]{1,0:T(8,128)} copy(f32[4096,384]{0,1:T(8,128)} %get-tuple-element.466) | data formatting | bytes 12582912 | tf_op jit(solution)/shard_map/while/body/eval_jaxpr/dot_general | solution.py:86
  283.1 6.8 %fusion.169 = f32[3,4096]{1,0:T(4,128)S(1)} fusion(f32[4096,384]{1,0:T(8,128)} %copy.331, bf16[3,2,4096,384]{3,2,1,0:T(8,128)(2,1)} %get-tuple-element.521, s32[]{:T(128)} %get-tuple-element.495), kind=kLoop, calls=%fused_computation.2.clone.1 | loop fusion | flops 14143488 | bytes 15777796 | tf_op jit(solution)/shard_map/while/body/eval_jaxpr/reduce_sum | solution.py:88
  290.4 9.9 %fusion.170 = f32[4096,384]{1,0:T(8,128)S(1)} fusion(f32[3,4096]{1,0:T(4,128)S(1)} %broadcast_multiply_fusion.5, bf16[3,2,4096,384]{3,2,1,0:T(8,128)(2,1)} %get-tuple-element.521, s32[]{:T(128)} %get-tuple-element.495), kind=kLoop, calls=%fused_computation.3.clone.1 | loop fusion | flops 12582912 | bytes 15777796 | tf_op jit(solution)/shard_map/while/body/eval_jaxpr/reduce_sum | solution.py:93
  300.4 3.2 fusion.172
  303.6 1.4 copy.332
  305.5 3.0 fusion.174
  308.6 0.6 copy-done.12
  309.2 1.3 dynamic_slice.135
  313.1 0.7 dynamic-slice_bitcast_fusion.5
  313.8 2.2 constant_dynamic-slice_fusion.2
  316.0 3.0 copy.330
  319.0 7.4 %multiply_reduce_fusion.4 = (f32[4096]{0:T(1024)S(1)}, f32[4096,384]{0,1:T(8,128)}) fusion(bf16[1,4096,384]{1,2,0:T(8,128)(2,1)} %copy.330, s32[]{:T(128)S(6)} %select_n.130, bf16[256,256]{1,0:T(8,128)(2,1)} %get-tuple-element.462, bf16[256,256]{1,0:T(8,128)(2,1)S(1)} %get-tuple-element.463, bf16[256,256]{1,0:T(8,128)(2,1)S(1)} %get-tuple-element.464, ...), kind=kOutput, calls=%fused_computation.6.clone.1 | convolution fusion | flops 1213853696 | bytes 13123588 | tf_op jit(solution)/shard_map/while/body/eval_jaxpr/dot_general | solution.py:86
  326.4 6.6 %copy.331 = f32[4096,384]{1,0:T(8,128)} copy(f32[4096,384]{0,1:T(8,128)} %get-tuple-element.466) | data formatting | bytes 12582912 | tf_op jit(solution)/shard_map/while/body/eval_jaxpr/dot_general | solution.py:86
  332.9 6.8 %fusion.169 = f32[3,4096]{1,0:T(4,128)S(1)} fusion(f32[4096,384]{1,0:T(8,128)} %copy.331, bf16[3,2,4096,384]{3,2,1,0:T(8,128)(2,1)} %get-tuple-element.521, s32[]{:T(128)} %get-tuple-element.495), kind=kLoop, calls=%fused_computation.2.clone.1 | loop fusion | flops 14143488 | bytes 15777796 | tf_op jit(solution)/shard_map/while/body/eval_jaxpr/reduce_sum | solution.py:88
  340.2 9.9 %fusion.170 = f32[4096,384]{1,0:T(8,128)S(1)} fusion(f32[3,4096]{1,0:T(4,128)S(1)} %broadcast_multiply_fusion.5, bf16[3,2,4096,384]{3,2,1,0:T(8,128)(2,1)} %get-tuple-element.521, s32[]{:T(128)} %get-tuple-element.495), kind=kLoop, calls=%fused_computation.3.clone.1 | loop fusion | flops 12582912 | bytes 15777796 | tf_op jit(solution)/shard_map/while/body/eval_jaxpr/reduce_sum | solution.py:93
  350.2 3.2 fusion.172
  353.4 1.4 copy.332
  355.3 3.0 fusion.174
  358.4 0.6 copy-done.12
  359.0 2.6 convert_element_type.116
  361.7 1.7 copy.273
  363.5 30.4 %reduce-scatter.3.cloned.1.call-done = bf16[2,6,3,32,256]{4,3,2,1,0:T(8,128)(2,1)} async-done(((bf16[8,6,3,32,256]{4,3,2,1,0:T(8,128)(2,1)}), bf16[2,6,3,32,256]{4,3,2,1,0:T(8,128)(2,1)}) %reduce-scatter.3.cloned.1.call-update) | async-done | bytes 589840 | tf_op jit(solution)/shard_map/reduce_scatter | solution.py:62
  393.9 21.4 %reduce-scatter.5.cloned.1.call-done = bf16[1,6,3,32,256]{4,3,2,1,0:T(8,128)(2,1)} async-done(((bf16[2,6,3,32,256]{4,3,2,1,0:T(8,128)(2,1)}), bf16[1,6,3,32,256]{4,3,2,1,0:T(8,128)(2,1)}) %reduce-scatter.5.cloned.1.call-update) | async-done | bytes 294928 | tf_op jit(solution)/shard_map/reduce_scatter | solution.py:62
  415.3 0.8 slice_bitcast_fusion.48
  416.2 3.8 collective-permute-start.6
  420.0 0.7 copy.277
  420.7 1.9 collective-permute-start.7
  422.6 1.0 convert_element_type.117
  423.7 2.4 collective-permute-done.7
  426.3 0.9 copy.278
  (94 shorter events, 10.2 us)
Async XLA Ops:
  7.2 97.1 %all-gather.3.cloned.1.call-start = ((), (), s32[]{:S(2)}) async-start(), calls=%async_computation.3 | async-start | bytes 5898240 | tf_op jit(solution)/shard_map/all_gather | solution.py:163
  8.0 207.7 %copy-start.9 = (pred[4,5]{0,1:T(8,128)(4,1)}, pred[4,5]{0,1:T(8,128)(4,1)S(1)}, u32[]{:S(2)}) copy-start(pred[4,5]{0,1:T(8,128)(4,1)S(1)} %copy.226) | copy-start | bytes 64
  9.1 6.7 %collective-permute-start = (bf16[2,5,32,256]{3,2,0,1:T(8,128)(2,1)S(1)}, bf16[2,5,32,256]{3,2,0,1:T(8,128)(2,1)S(1)}, u32[]{:S(2)}, u32[]{:S(2)}) collective-permute-start(bf16[2,5,32,256]{3,2,0,1:T(8,128)(2,1)S(1)} %get-tuple-element.389), channel_id=1, source_target_pairs={{0,8},{8,16},{16,24},{24,32},{32,40},{40,48},{48,56},{56,64},{64,7... | collective-permute-start | bytes 491528 | tf_op jit(solution)/shard_map/ppermute | solution.py:31
  13.6 6.6 %collective-permute-start.1 = (bf16[2,5,32,256]{3,2,0,1:T(8,128)(2,1)S(1)}, bf16[2,5,32,256]{3,2,0,1:T(8,128)(2,1)S(1)}, u32[]{:S(2)}, u32[]{:S(2)}) collective-permute-start(bf16[2,5,32,256]{3,2,0,1:T(8,128)(2,1)S(1)} %get-tuple-element.390), channel_id=1, source_target_pairs={{8,0},{16,8},{24,16},{32,24},{40,32},{48,40},{56,48},{64,56},{72,6... | collective-permute-start | bytes 491528 | tf_op jit(solution)/shard_map/ppermute | solution.py:33
  21.2 184.3 %all-gather.5.cloned.1.call-start = ((), (), s32[]{:S(2)}) async-start(), calls=%async_computation.4 | async-start | bytes 5898240 | tf_op jit(solution)/shard_map/all_gather | solution.py:163
  109.7 2.5 copy-start.1
  115.1 6.6 %collective-permute-start.2 = (bf16[2,5,32,256]{3,2,0,1:T(8,128)(2,1)S(1)}, bf16[2,5,32,256]{3,2,0,1:T(8,128)(2,1)S(1)}, u32[]{:S(2)}, u32[]{:S(2)}) collective-permute-start(bf16[2,5,32,256]{3,2,0,1:T(8,128)(2,1)S(1)} %get-tuple-element.387), channel_id=1, source_target_pairs={{0,8},{8,16},{16,24},{24,32},{32,40},{40,48},{48,56},{56,64},{64,7... | collective-permute-start | bytes 491528 | tf_op jit(solution)/shard_map/ppermute | solution.py:31
  119.5 6.6 %collective-permute-start.3 = (bf16[2,5,32,256]{3,2,0,1:T(8,128)(2,1)S(1)}, bf16[2,5,32,256]{3,2,0,1:T(8,128)(2,1)S(1)}, u32[]{:S(2)}, u32[]{:S(2)}) collective-permute-start(bf16[2,5,32,256]{3,2,0,1:T(8,128)(2,1)S(1)} %get-tuple-element.388), channel_id=1, source_target_pairs={{8,0},{16,8},{24,16},{32,24},{40,32},{48,40},{56,48},{64,56},{72,6... | collective-permute-start | bytes 491528 | tf_op jit(solution)/shard_map/ppermute | solution.py:33
  127.1 266.9 %reduce-scatter.3.cloned.1.call-start = ((), (), s32[]{:S(2)}) async-start(), calls=%async_computation.5 | async-start | bytes 2949120 | tf_op jit(solution)/shard_map/reduce_scatter | solution.py:62
  210.9 2.5 copy-start.2
  216.3 24.4 %copy-start.6 = (bf16[4,5,32,256]{3,2,0,1:T(8,128)(2,1)}, bf16[4,5,32,256]{3,2,0,1:T(8,128)(2,1)S(1)}, u32[]{:S(2)}) copy-start(bf16[4,5,32,256]{3,2,0,1:T(8,128)(2,1)S(1)} %fusion.119) | copy-start | bytes 983044
  240.8 14.3 %copy-start.5 = (bf16[8,4,3,32,256]{4,3,0,2,1:T(8,128)(2,1)}, bf16[8,4,3,32,256]{4,3,0,2,1:T(8,128)(2,1)S(1)}, u32[]{:S(2)}) copy-start(bf16[8,4,3,32,256]{4,3,0,2,1:T(8,128)(2,1)S(1)} %copy.326) | copy-start | bytes 4718596
  240.9 9.8 %collective-permute-start.4 = (bf16[1,3,256,256]{3,2,1,0:T(8,128)(2,1)S(1)}, bf16[1,3,256,256]{3,2,1,0:T(8,128)(2,1)S(1)}, u32[]{:S(2)}, u32[]{:S(2)}) collective-permute-start(bf16[1,3,256,256]{3,2,1,0:T(8,128)(2,1)S(1)} %bitcast.239), channel_id=1, source_target_pairs={{0,8},{8,16},{16,24},{24,32},{32,40},{40,48},{48,56},{56,64},{64,7... | collective-permute-start | bytes 1179656 | tf_op jit(solution)/shard_map/ppermute | solution.py:31
  246.0 9.1 %collective-permute-start.5 = (bf16[1,3,256,256]{3,2,1,0:T(8,128)(2,1)S(1)}, bf16[1,3,256,256]{3,2,1,0:T(8,128)(2,1)S(1)}, u32[]{:S(2)}, u32[]{:S(2)}) collective-permute-start(bf16[1,3,256,256]{3,2,1,0:T(8,128)(2,1)S(1)} %bitcast.238), channel_id=1, source_target_pairs={{8,0},{16,8},{24,16},{32,24},{40,32},{48,40},{56,48},{64,56},{72,6... | collective-permute-start | bytes 1179656 | tf_op jit(solution)/shard_map/ppermute | solution.py:33
  259.4 4.6 %copy-start.3 = (bf16[6,3,256,256]{3,2,1,0:T(8,128)(2,1)}, bf16[6,3,256,256]{3,2,1,0:T(8,128)(2,1)S(1)}, u32[]{:S(2)}) copy-start(bf16[6,3,256,256]{3,2,1,0:T(8,128)(2,1)S(1)} %get-tuple-element.520) | copy-start | bytes 7077892 | tf_op jit(solution)/shard_map/while
  283.1 6.9 %copy-start.8 = (f32[2,4096]{1,0:T(2,128)S(1)}, f32[2,4096]{1,0:T(2,128)}, u32[]{:S(2)}) copy-start(f32[2,4096]{1,0:T(2,128)} %get-tuple-element.522) | copy-start | bytes 98308 | tf_op jit(solution)/shard_map/while
  303.6 1.5 copy-start
  305.4 3.0 copy-start.11
  305.5 3.7 copy-start.4
  308.6 0.6 copy-start.12
  309.2 4.6 %copy-start.3 = (bf16[6,3,256,256]{3,2,1,0:T(8,128)(2,1)}, bf16[6,3,256,256]{3,2,1,0:T(8,128)(2,1)S(1)}, u32[]{:S(2)}) copy-start(bf16[6,3,256,256]{3,2,1,0:T(8,128)(2,1)S(1)} %get-tuple-element.520) | copy-start | bytes 7077892 | tf_op jit(solution)/shard_map/while
  332.9 6.9 %copy-start.8 = (f32[2,4096]{1,0:T(2,128)S(1)}, f32[2,4096]{1,0:T(2,128)}, u32[]{:S(2)}) copy-start(f32[2,4096]{1,0:T(2,128)} %get-tuple-element.522) | copy-start | bytes 98308 | tf_op jit(solution)/shard_map/while
  353.4 1.5 copy-start
  355.3 3.0 copy-start.11
  355.3 3.7 copy-start.4
  358.4 0.6 copy-start.12
  363.4 56.6 %copy-start.7 = (bf16[4,5,32,256]{3,2,0,1:T(8,128)(2,1)S(1)}, bf16[4,5,32,256]{3,2,0,1:T(8,128)(2,1)}, u32[]{:S(2)}) copy-start(bf16[4,5,32,256]{3,2,0,1:T(8,128)(2,1)} %copy-done.6) | copy-start | bytes 983044
  363.4 62.8 %copy-start.10 = (pred[4,5]{0,1:T(8,128)(4,1)S(1)}, pred[4,5]{0,1:T(8,128)(4,1)}, u32[]{:S(2)}) copy-start(pred[4,5]{0,1:T(8,128)(4,1)} %copy-done.9) | copy-start | bytes 64
  363.4 51.9 %reduce-scatter.5.cloned.1.call-start = ((), (), s32[]{:S(2)}) async-start(), calls=%async_computation.6 | async-start | bytes 884736 | tf_op jit(solution)/shard_map/reduce_scatter | solution.py:62
  416.2 7.5 %collective-permute-start.6 = (bf16[3,32,256]{2,1,0:T(8,128)(2,1)S(1)}, bf16[3,32,256]{2,1,0:T(8,128)(2,1)S(1)}, u32[]{:S(2)}, u32[]{:S(2)}) collective-permute-start(bf16[3,32,256]{2,1,0:T(8,128)(2,1)S(1)} %get-tuple-element.391), channel_id=1, source_target_pairs={{0,8},{8,16},{16,24},{24,32},{32,40},{40,48},{48,56},{56,64},{64,7... | collective-permute-start | bytes 147464 | tf_op jit(solution)/shard_map/ppermute | solution.py:20
  420.7 5.4 %collective-permute-start.7 = (bf16[3,32,256]{2,1,0:T(8,128)(2,1)S(1)}, bf16[3,32,256]{2,1,0:T(8,128)(2,1)S(1)}, u32[]{:S(2)}, u32[]{:S(2)}) collective-permute-start(bf16[3,32,256]{2,1,0:T(8,128)(2,1)S(1)} %get-tuple-element.392), channel_id=1, source_target_pairs={{8,0},{16,8},{24,16},{32,24},{40,32},{48,40},{56,48},{64,56},{72,6... | collective-permute-start | bytes 147464 | tf_op jit(solution)/shard_map/ppermute | solution.py:20
Sparse Core Ops, SparseCore 0:
  21.3 82.8 all-gather.2
  127.2 78.2 all-gather.4
  363.5 30.3 reduce-scatter.2
  396.1 19.1 reduce-scatter.4
where the time goes:
time: 435 us; the launch traced here: 434 us
  waiting for transfers between devices  232 us (53%)
  local copies, waits for them, and re-layouts  52 us (12%)
  other arithmetic  49.8 us (11%)
  matrix products  30.2 us (7%)
  starting transfers between devices  25.8 us (6%)
  blocking collectives  24.1 us (6%)
  between operations  14.1 us (3%)
  loops' own time  5.52 us (1%)
    all_gather x2, waiting for transfers between devices, on_device(): right_full = lax.all_gather(near_right, COL, axis=2, tiled=True)  161 us
    reduce_scatter x2, waiting for transfers between devices, sum_in_order(): pieces = lax.psum_scatter(pieces, axes[k], scatter_dimension=0, tiled=True)  51.8 us
    all_to_all x1, blocking collectives, sent_to_all(): lax.all_to_all(jnp.broadcast_to(value[None], (length, *value.shape)), axi...  24.1 us
    reduce_sum x2, other arithmetic, tile_terms(): jnp.sum(((2.0 * by_gradient * scaled)[None] * slopes)[:, :, None] * grads...  19.9 us
    dot_general x2, matrix products, tile_terms(): jnp.dot(values, window_block, preferred_element_type=jnp.float32)  14.7 us
    ppermute x3, starting transfers between devices, padded(): lax.ppermute(tail, axis, [(i, (i + 1) % count) for i in range(ends)])  14 us
    reduce_sum x2, other arithmetic, tile_terms(): jnp.sum(projected[None] * grads.astype(jnp.float32), axis=2)  13.6 us
    ppermute x3, waiting for transfers between devices, padded(): lax.ppermute(head, axis, [((i + 1) % count, i) for i in range(ends)])  13.2 us
  transfers between devices with their start and end apart: 12, of which 11 were waited for; matrix products, arithmetic and copies ran while one was open for 0% of the time, Pallas kernels for 0%

commit v1 on v0

--- a/solution.py
+++ b/solution.py
@@ -1,6 +1,8 @@
 import jax
 import jax.numpy as jnp
 from jax import lax
+from jax.experimental import pallas as pl
+from jax.experimental.pallas import tpu as pltpu
 from jax.sharding import Mesh
 from jax.sharding import PartitionSpec as P
 
@@ -73,32 +75,109 @@
     return sum_in_order(cut_along(value, dim, length), axes, sequence)
 
 
-def energy_sum(point_density, grad_square):
-    spread = jnp.sqrt(point_density * point_density + 1.0)
-    reduced = grad_square / spread ** (8.0 / 3.0)
-    enhance = 1.0 + kappa_pbe - kappa_pbe / (1.0 + mu_pbe * reduced / kappa_pbe)
-    return jnp.sum(-slater_cx * spread ** (4.0 / 3.0) * enhance)
-
-
-def tile_terms(values, grads, quadrature, window_block):
-    functions = values.shape[1]
-    points = values.shape[0]
-    projected = jnp.dot(values, window_block, preferred_element_type=jnp.float32)
-    point_density = jnp.sum(projected * values.astype(jnp.float32), axis=1) / functions
-    slopes = 2.0 * jnp.sum(projected[None] * grads.astype(jnp.float32), axis=2) / functions
-    grad_square = jnp.sum(slopes * slopes, axis=0)
-    by_density, by_gradient = jax.grad(energy_sum, argnums=(0, 1))(point_density, grad_square)
-    scaled = quadrature / points
-    weighted = (0.5 * by_density * scaled)[:, None] * values.astype(jnp.float32)
-    weighted = weighted + jnp.sum(
-        ((2.0 * by_gradient * scaled)[None] * slopes)[:, :, None] * grads.astype(jnp.float32),
-        axis=0,
-    )
-    weighted = weighted.astype(jnp.bfloat16)
+POINT_BLOCK = 1024
+CHUNK = 128
+
+
+def potentials(density, grad_square):
+    inverse_root = jnp.exp(jnp.log(density * density + 1.0) * (-1.0 / 3.0))
+    inverse_two = inverse_root * inverse_root
+    reduced = grad_square * (inverse_two * inverse_two)
+    share = 1.0 / (1.0 + (mu_pbe / kappa_pbe) * reduced)
+    enhance = 1.0 + kappa_pbe - kappa_pbe * share
+    slope = mu_pbe * share * share
+    by_density = (-slater_cx * 4.0 / 3.0) * inverse_root * density * (enhance - 2.0 * reduced * slope)
+    by_gradient = -slater_cx * slope * inverse_two
+    return by_density, by_gradient
+
+
+def tile_kernel(window_ref, values_ref, grads_ref, weights_ref, density_ref, term_ref, projected, weighted, total):
+    step = pl.program_id(1)
+    functions = values_ref.shape[2]
+    projected[...] = jnp.dot(values_ref[0], window_ref[0], preferred_element_type=jnp.float32)
+    lane = lax.broadcasted_iota(jnp.int32, (8, 128), 1)
+    packed = [jnp.zeros((8, 128), jnp.float32) for _ in range(4)]
+    for chunk in range(POINT_BLOCK // CHUNK):
+        rows = slice(chunk * CHUNK, (chunk + 1) * CHUNK)
+        x = projected[rows, :]
+        for k in range(4):
+            basis = values_ref[0, rows, :] if k == 0 else grads_ref[k - 1, 0, rows, :]
+            sums = jnp.sum(x * basis.astype(jnp.float32), axis=1, keepdims=True)
+            for group in range(CHUNK // 8):
+                here = chunk * (CHUNK // 8) + group
+                packed[k] = jnp.where(lane == here, sums[8 * group : 8 * group + 8], packed[k])
+    density = packed[0] / functions
+    slopes = [2.0 * packed[k] / functions for k in (1, 2, 3)]
+    grad_square = slopes[0] * slopes[0] + slopes[1] * slopes[1] + slopes[2] * slopes[2]
+    by_density, by_gradient = potentials(density, grad_square)
+    density_ref[0, 0] = density
+    scaled = weights_ref[0, 0] * (1.0 / 4096.0)
+    factors = [0.5 * by_density * scaled] + [2.0 * by_gradient * scaled * s for s in slopes]
+    for pair in range(POINT_BLOCK // 16):
+        rows = slice(pair * 16, pair * 16 + 16)
+        z = None
+        for k in range(4):
+            basis = values_ref[0, rows, :] if k == 0 else grads_ref[k - 1, 0, rows, :]
+            column = jnp.concatenate(
+                [factors[k][:, 2 * pair : 2 * pair + 1], factors[k][:, 2 * pair + 1 : 2 * pair + 2]], axis=0
+            )
+            part = column * basis.astype(jnp.float32)
+            z = part if z is None else z + part
+        weighted[rows, :] = z.astype(jnp.bfloat16)
     one_side = lax.dot_general(
-        values, weighted, (((0,), (0,)), ((), ())), preferred_element_type=jnp.float32
-    )
-    return (point_density, one_side + one_side.T)
+        values_ref[0], weighted[...], (((0,), (0,)), ((), ())), preferred_element_type=jnp.float32
+    )
+
+    @pl.when(step == 0)
+    def _():
+        total[...] = one_side
+
+    @pl.when(step > 0)
+    def _():
+        total[...] += one_side
+
+    @pl.when(step == pl.num_programs(1) - 1)
+    def _():
+        term_ref[0] = total[...] + total[...].T
+
+
+def tile_terms(values, grads, quadrature, window_blocks):
+    tiles, points, functions = values.shape
+    steps = points // POINT_BLOCK
+    packed_weights = jnp.swapaxes(quadrature.reshape(tiles, steps, 128, 8), 2, 3)
+    density, terms = pl.pallas_call(
+        tile_kernel,
+        name="tile_terms",
+        grid=(tiles, steps),
+        in_specs=[
+            pl.BlockSpec((1, functions, functions), lambda t, s: (t, 0, 0)),
+            pl.BlockSpec((1, POINT_BLOCK, functions), lambda t, s: (t, s, 0)),
+            pl.BlockSpec((3, 1, POINT_BLOCK, functions), lambda t, s: (0, t, s, 0)),
+            pl.BlockSpec((1, 1, 8, 128), lambda t, s: (t, s, 0, 0)),
+        ],
+        out_specs=[
+            pl.BlockSpec((1, 1, 8, 128), lambda t, s: (t, s, 0, 0)),
+            pl.BlockSpec((1, functions, functions), lambda t, s: (t, 0, 0)),
+        ],
+        out_shape=[
+            jax.ShapeDtypeStruct((tiles, steps, 8, 128), jnp.float32),
+            jax.ShapeDtypeStruct((tiles, functions, functions), jnp.float32),
+        ],
+        scratch_shapes=[
+            pltpu.VMEM((POINT_BLOCK, functions), jnp.float32),
+            pltpu.VMEM((POINT_BLOCK, functions), jnp.bfloat16),
+            pltpu.VMEM((functions, functions), jnp.float32),
+        ],
+        compiler_params=pltpu.CompilerParams(
+            dimension_semantics=("arbitrary", "arbitrary"), vmem_limit_bytes=40 * 1024 * 1024
+        ),
+        cost_estimate=pl.CostEstimate(
+            flops=4 * tiles * points * functions * functions,
+            bytes_accessed=8 * tiles * points * functions,
+            transcendentals=0,
+        ),
+    )(window_blocks, values, grads, packed_weights)
+    return jnp.swapaxes(density, 2, 3).reshape(tiles, points), terms
 
 
 def band_product(left, right_padded):
@@ -169,29 +248,16 @@
     rows_band = gather_directly(current[:, 1:4], COL, 2)
     near = padded(rows_band, (("row", 0),), 1)
     tiles_here = windows.shape[0]
-    points = basis_values.shape[1]
     block_size = near.shape[2]
-
-    def one_tile(tile_index, carry):
-        summed, densities = carry
-        position = tile_index.astype(jnp.int32)
-        start_step = windows[position]
-        lead = start_step // 2 - (band_rows * row_index - 1)
-        offset = start_step % 2 * step_size
-        window_block = window_of(near, lead, offset, functions)
-        values = lax.dynamic_index_in_dim(basis_values, position, 0, keepdims=False)
-        grads = lax.dynamic_index_in_dim(basis_grads, position, 1, keepdims=False)
-        quadrature = lax.dynamic_index_in_dim(weights, position, 0, keepdims=False)
-        point_density, contribution = tile_terms(values, grads, quadrature, window_block)
-        summed = spread_term(summed, contribution, lead, offset)
-        densities = lax.dynamic_update_index_in_dim(densities, point_density, position, 0)
-        return (summed, densities)
-
-    start_carry = (
-        jnp.zeros((band_rows + 2, 3, block_size, block_size), jnp.float32),
-        jnp.zeros((tiles_here, points), jnp.float32),
-    )
-    local_terms, densities = lax.fori_loop(0, tiles_here, one_tile, start_carry)
+    leads = [windows[t] // 2 - (band_rows * row_index - 1) for t in range(tiles_here)]
+    offsets = [windows[t] % 2 * step_size for t in range(tiles_here)]
+    window_blocks = jnp.stack(
+        [window_of(near, leads[t], offsets[t], functions) for t in range(tiles_here)]
+    )
+    densities, contributions = tile_terms(basis_values, basis_grads, weights, window_blocks)
+    local_terms = jnp.zeros((band_rows + 2, 3, block_size, block_size), jnp.float32)
+    for t in range(tiles_here):
+        local_terms = spread_term(local_terms, contributions[t], leads[t], offsets[t])
     owner_part = scatter_axes(local_terms.astype(jnp.bfloat16), COL, (1, 0), 2).astype(jnp.float32)
     mine = edge_rows(owner_part)
     xc_matrix = jnp.where(kept, jnp.pad(mine, ((0, 0), (1, 1), (0, 0), (0, 0))), 0.0)

time: 435 us -> 362 us (0.83)
  other arithmetic: 49.8 us -> 10.6 us
  local copies, waits for them, and re-layouts: 52 us -> 22.4 us
  Pallas kernels: 0 us -> 22.8 us
  matrix products: 30.2 us -> 9.05 us
  waiting for transfers between devices: 232 us -> 226 us
  loops' own time: 5.52 us -> 0 us
  between operations: 14.1 us -> 19.5 us
    reduce_sum x6 -> x0, other arithmetic: 33.6 us -> none  [the longest x2 19.9 us: tile_terms(): jnp.sum(((2.0 * by_gradient * scaled)[None] * slopes)[:, :, None] * grads...]
    pallas_call x0 -> x1, Pallas kernels: none -> 22.8 us  [tile_terms(): pl.pallas_call(tile_kernel, name='tile_terms', grid=(tiles, steps), in_sp...]
    dot_general x4 -> x0, matrix products: 21.1 us -> none  [the longest x2 14.7 us: tile_terms(): jnp.dot(values, window_block, preferred_element_type=jnp.float32)]
    dot_general x4 -> x0, local copies, waits for them, and re-layouts: 15.8 us -> none  [the longest x2 13.1 us: tile_terms(): jnp.dot(values, window_block, preferred_element_type=jnp.float32)]
    dynamic_slice x6 -> x0, local copies, waits for them, and re-layouts: 13 us -> none  [the longest x4 10.4 us: one_tile(): values = lax.dynamic_index_in_dim(basis_values, position, 0, keepdims=False)]
    another operation x1 -> x0, loops' own time: 5.52 us -> none  [on_device(): local_terms, densities = lax.fori_loop(0, tiles_here, one_tile, start_carry)]
    dynamic_update_slice x2, other arithmetic: 5.9 us -> 0.52 us  [spread_term(): return lax.dynamic_update_slice_in_dim(summed, paired + increment, lead, 0)]
  transfers between devices with their start and end apart: 12 -> 12, of which waited for: 11 -> 10; matrix products, arithmetic and copies ran while one was open for 0% -> 1% of each run, Pallas kernels for 0% -> 0%
where the time goes in v1:
time: 362 us; the launch traced here: 360 us
  waiting for transfers between devices  226 us (62%)
  starting transfers between devices  25.8 us (7%)
  blocking collectives  24.1 us (7%)
  Pallas kernels  22.8 us (6%)
  local copies, waits for them, and re-layouts  22.4 us (6%)
  between operations  19.5 us (5%)
  other arithmetic  10.6 us (3%)
  matrix products  9.05 us (3%)
    all_gather x2, waiting for transfers between devices, on_device(): right_full = lax.all_gather(near_right, COL, axis=2, tiled=True)  161 us
    reduce_scatter x2, waiting for transfers between devices, sum_in_order(): pieces = lax.psum_scatter(pieces, axes[k], scatter_dimension=0, tiled=True)  52 us
    all_to_all x1, blocking collectives, sent_to_all(): lax.all_to_all(jnp.broadcast_to(value[None], (length, *value.shape)), axi...  24.1 us
    pallas_call x1, Pallas kernels, tile_terms(): pl.pallas_call(tile_kernel, name='tile_terms', grid=(tiles, steps), in_sp...  22.8 us
    ppermute x3, starting transfers between devices, padded(): lax.ppermute(tail, axis, [(i, (i + 1) % count) for i in range(ends)])  13.9 us
    ppermute x3, waiting for transfers between devices, padded(): lax.ppermute(head, axis, [((i + 1) % count, i) for i in range(ends)])  9.78 us
    dot_general x20, matrix products, band_product(): jnp.einsum('brk,bdkc->bdrc', left[:, offset_step], picked, preferred_elem...  9.05 us
    slice x2, local copies, waits for them, and re-layouts, band_product(): shifted = right_padded[offset_step:offset_step + blocks]  8.97 us
  transfers between devices with their start and end apart: 12, of which 10 were waited for; matrix products, arithmetic and copies ran while one was open for 1% of the time, Pallas kernels for 0%

profile of v1, /device:TPU:1, one launch (start us, length us, event | category | flops | bytes accessed | tf_op | source)
XLA Modules:
  0.0 360.5 jit_solution(8294242820097658001)
XLA Ops:
  7.2 0.7 broadcast_compare_fusion
  8.0 1.1 copy_select_fusion
  9.1 4.5 %collective-permute-start = (bf16[2,5,32,256]{3,2,0,1:T(8,128)(2,1)S(1)}, bf16[2,5,32,256]{3,2,0,1:T(8,128)(2,1)S(1)}, u32[]{:S(2)}, u32[]{:S(2)}) collective-permute-start(bf16[2,5,32,256]{3,2,0,1:T(8,128)(2,1)S(1)} %get-tuple-element.52), channel_id=1, source_target_pairs={{0,8},{8,16},{16,24},{24,32},{32,40},{40,48},{48,56},{56,64},{64,7... | collective-permute-start | bytes 491528 | tf_op jit(solution)/shard_map/ppermute | solution.py:33
  13.6 1.9 collective-permute-start.1
  15.5 0.3 collective-permute-done
  15.9 4.4 %collective-permute-done.1 = bf16[2,5,32,256]{3,2,0,1:T(8,128)(2,1)S(1)} collective-permute-done((bf16[2,5,32,256]{3,2,0,1:T(8,128)(2,1)S(1)}, bf16[2,5,32,256]{3,2,0,1:T(8,128)(2,1)S(1)}, u32[]{:S(2)}, u32[]{:S(2)}) %collective-permute-start.1) | collective-permute-done | bytes 163872 | tf_op jit(solution)/shard_map/ppermute | solution.py:35
  20.3 0.9 pad_maximum_fusion.5
  21.2 83.0 %all-gather.3.cloned.1.call-done = bf16[8,5,256,256]{3,2,0,1:T(8,128)(2,1)} async-done(((bf16[8,5,32,256]{3,2,0,1:T(8,128)(2,1)}), bf16[8,5,256,256]{3,2,0,1:T(8,128)(2,1)}) %all-gather.3.cloned.1.call-update) | async-done | bytes 5242896 | tf_op jit(solution)/shard_map/all_gather | solution.py:242
  104.3 4.5 %fusion.149 = (bf16[4,5,256,256]{3,2,0,1:T(8,128)(2,1)S(1)}, bf16[4,5,256,256]{3,2,0,1:T(8,128)(2,1)S(1)}, bf16[4,5,256,256]{3,2,0,1:T(8,128)(2,1)S(1)}, bf16[4,5,256,256]{3,2,0,1:T(8,128)(2,1)S(1)}) fusion(bf16[8,5,256,256]{3,2,0,1:T(8,128)(2,1)} %all-gather.3.cloned.1.call-done), kind=kLoop, calls=%fused_computation.169 | loop fusion | bytes 20971520 | tf_op jit(solution)/shard_map/slice | solution.py:187
  108.7 0.5 fusion.10
  109.2 0.5 fusion.12
  109.7 0.4 fusion.14
  110.1 0.4 fusion.40
  110.5 1.7 copy-done
  112.2 0.5 fusion.110
  112.7 0.5 fusion.11
  113.2 0.5 fusion.13
  113.6 0.4 fusion.15
  114.1 0.4 fusion.39
  114.5 0.5 fusion.95
  115.0 4.4 %collective-permute-start.2 = (bf16[2,5,32,256]{3,2,0,1:T(8,128)(2,1)S(1)}, bf16[2,5,32,256]{3,2,0,1:T(8,128)(2,1)S(1)}, u32[]{:S(2)}, u32[]{:S(2)}) collective-permute-start(bf16[2,5,32,256]{3,2,0,1:T(8,128)(2,1)S(1)} %get-tuple-element.50), channel_id=1, source_target_pairs={{0,8},{8,16},{16,24},{24,32},{32,40},{40,48},{48,56},{56,64},{64,7... | collective-permute-start | bytes 491528 | tf_op jit(solution)/shard_map/ppermute | solution.py:33
  119.4 1.9 collective-permute-start.3
  121.3 0.3 collective-permute-done.2
  121.7 4.4 %collective-permute-done.3 = bf16[2,5,32,256]{3,2,0,1:T(8,128)(2,1)S(1)} collective-permute-done((bf16[2,5,32,256]{3,2,0,1:T(8,128)(2,1)S(1)}, bf16[2,5,32,256]{3,2,0,1:T(8,128)(2,1)S(1)}, u32[]{:S(2)}, u32[]{:S(2)}) %collective-permute-start.3) | collective-permute-done | bytes 163872 | tf_op jit(solution)/shard_map/ppermute | solution.py:35
  126.1 0.9 pad_maximum_fusion.6
  127.0 78.4 %all-gather.5.cloned.1.call-done = bf16[8,5,256,256]{3,2,0,1:T(8,128)(2,1)} async-done(((bf16[8,5,32,256]{3,2,0,1:T(8,128)(2,1)}), bf16[8,5,256,256]{3,2,0,1:T(8,128)(2,1)}) %all-gather.5.cloned.1.call-update) | async-done | bytes 5242896 | tf_op jit(solution)/shard_map/all_gather | solution.py:242
  205.4 4.5 %fusion.148 = (bf16[4,5,256,256]{3,2,0,1:T(8,128)(2,1)S(1)}, bf16[4,5,256,256]{3,2,0,1:T(8,128)(2,1)S(1)}, bf16[4,5,256,256]{3,2,0,1:T(8,128)(2,1)S(1)}, bf16[4,5,256,256]{3,2,0,1:T(8,128)(2,1)S(1)}) fusion(bf16[8,5,256,256]{3,2,0,1:T(8,128)(2,1)} %all-gather.5.cloned.1.call-done), kind=kLoop, calls=%fused_computation.168 | loop fusion | bytes 20971520 | tf_op jit(solution)/shard_map/slice | solution.py:187
  209.9 0.5 fusion.18
  210.4 0.5 fusion.20
  210.8 0.4 fusion.22
  211.2 0.4 fusion.38
  211.6 1.7 copy-done.1
  213.3 0.5 fusion.107
  213.9 0.5 fusion.19
  214.3 0.5 fusion.21
  214.8 0.4 fusion.23
  215.2 0.4 fusion.37
  215.6 0.5 fusion.101
  216.4 24.1 %all_to_all.5 = bf16[8,4,3,32,256]{4,3,2,1,0:T(8,128)(2,1)S(1)} all-to-all(bf16[8,4,3,32,256]{4,3,2,1,0:T(8,128)(2,1)S(1)} %broadcast_in_dim.63), channel_id=1, replica_groups=mesh['row'=16,'col_0'=2,'col_1'=4] {'col_0','col_1'}, dimensions={0} | all-to-all | bytes 3145728 | tf_op jit(solution)/shard_map/all_to_all | solution.py:50
  240.7 1.2 copy-done.2
  241.9 0.9 fusion.150
  242.8 5.1 %collective-permute-start.4 = (bf16[1,3,256,256]{3,2,1,0:T(8,128)(2,1)}, bf16[1,3,256,256]{3,2,1,0:T(8,128)(2,1)S(1)}, u32[]{:S(2)}, u32[]{:S(2)}) collective-permute-start(bf16[1,3,256,256]{3,2,1,0:T(8,128)(2,1)} %bitcast.45), channel_id=1, source_target_pairs={{0,8},{8,16},{16,24},{24,32},{32,40},{40,48},{48,56},{56,64},{64,7... | collective-permute-start | bytes 1179656 | tf_op jit(solution)/shard_map/ppermute | solution.py:33
  247.8 2.1 collective-permute-start.5
  250.0 0.6 fusion.154
  255.8 0.3 reshape.41
  256.3 1.0 collective-permute-done.5
  257.3 2.0 pad_maximum_fusion
  259.3 2.7 fusion.123
  262.1 22.8 %tile_terms.1 = (f32[2,4,8,128]{3,2,1,0:T(8,128)S(1)}, f32[2,384,384]{2,1,0:T(8,128)S(1)}) custom-call(bf16[2,384,384]{2,1,0:T(8,128)(2,1)S(1)} %pad_maximum_fusion.7.window_ref, bf16[2,4096,384]{2,1,0:T(8,128)(2,1)S(1)} %bitcast.197, bf16[3,2,4096,384]{3,2,1,0:T(8,128)(2,1)} %grads_ref.1, f32[2,4,8,128]{3,2,1,0:T(8,128)S(1)} %bitcast.198), custom_call_target="tpu_custom_call" | custom-call | flops 4831838208 | bytes 25165824 | tf_op jit(solution)/shard_map/tile_terms/pallas_call | solution.py:148
  285.6 0.3 fusion.118
  285.9 0.5 broadcast_in_dim.62
  286.5 0.4 fusion.24
  286.9 0.3 convert_element_type.66
  287.2 1.7 copy.263
  289.0 30.7 %reduce-scatter.3.cloned.1.call-done = bf16[2,6,3,32,256]{4,3,2,1,0:T(8,128)(2,1)} async-done(((bf16[8,6,3,32,256]{4,3,2,1,0:T(8,128)(2,1)}), bf16[2,6,3,32,256]{4,3,2,1,0:T(8,128)(2,1)}) %reduce-scatter.3.cloned.1.call-update) | async-done | bytes 589840 | tf_op jit(solution)/shard_map/reduce_scatter | solution.py:64
  319.7 21.4 %reduce-scatter.5.cloned.1.call-done = bf16[1,6,3,32,256]{4,3,2,1,0:T(8,128)(2,1)} async-done(((bf16[2,6,3,32,256]{4,3,2,1,0:T(8,128)(2,1)}), bf16[1,6,3,32,256]{4,3,2,1,0:T(8,128)(2,1)}) %reduce-scatter.5.cloned.1.call-update) | async-done | bytes 294928 | tf_op jit(solution)/shard_map/reduce_scatter | solution.py:64
  341.1 0.8 slice_bitcast_fusion.52
  341.9 3.8 %collective-permute-start.6 = (bf16[3,32,256]{2,1,0:T(8,128)(2,1)S(1)}, bf16[3,32,256]{2,1,0:T(8,128)(2,1)S(1)}, u32[]{:S(2)}, u32[]{:S(2)}) collective-permute-start(bf16[3,32,256]{2,1,0:T(8,128)(2,1)S(1)} %get-tuple-element.54), channel_id=1, source_target_pairs={{0,8},{8,16},{16,24},{24,32},{32,40},{40,48},{48,56},{56,64},{64,7... | collective-permute-start | bytes 147464 | tf_op jit(solution)/shard_map/ppermute | solution.py:22
  345.7 0.7 copy.268
  346.6 0.9 reshape.45
  347.6 1.9 collective-permute-start.7
  349.5 1.0 convert_element_type.67
  350.5 2.4 collective-permute-done.7
  353.1 0.9 copy.269
  (44 shorter events, 2.1 us)
Async XLA Ops:
  7.2 97.1 %all-gather.3.cloned.1.call-start = ((), (), s32[]{:S(2)}) async-start(), calls=%async_computation.3 | async-start | bytes 5898240 | tf_op jit(solution)/shard_map/all_gather | solution.py:242
  9.1 6.7 %collective-permute-start = (bf16[2,5,32,256]{3,2,0,1:T(8,128)(2,1)S(1)}, bf16[2,5,32,256]{3,2,0,1:T(8,128)(2,1)S(1)}, u32[]{:S(2)}, u32[]{:S(2)}) collective-permute-start(bf16[2,5,32,256]{3,2,0,1:T(8,128)(2,1)S(1)} %get-tuple-element.52), channel_id=1, source_target_pairs={{0,8},{8,16},{16,24},{24,32},{32,40},{40,48},{48,56},{56,64},{64,7... | collective-permute-start | bytes 491528 | tf_op jit(solution)/shard_map/ppermute | solution.py:33
  13.6 6.6 %collective-permute-start.1 = (bf16[2,5,32,256]{3,2,0,1:T(8,128)(2,1)S(1)}, bf16[2,5,32,256]{3,2,0,1:T(8,128)(2,1)S(1)}, u32[]{:S(2)}, u32[]{:S(2)}) collective-permute-start(bf16[2,5,32,256]{3,2,0,1:T(8,128)(2,1)S(1)} %get-tuple-element.53), channel_id=1, source_target_pairs={{8,0},{16,8},{24,16},{32,24},{40,32},{48,40},{56,48},{64,56},{72,6... | collective-permute-start | bytes 491528 | tf_op jit(solution)/shard_map/ppermute | solution.py:35
  21.2 184.2 %all-gather.5.cloned.1.call-start = ((), (), s32[]{:S(2)}) async-start(), calls=%async_computation.4 | async-start | bytes 5898240 | tf_op jit(solution)/shard_map/all_gather | solution.py:242
  109.7 2.5 copy-start
  115.0 6.6 %collective-permute-start.2 = (bf16[2,5,32,256]{3,2,0,1:T(8,128)(2,1)S(1)}, bf16[2,5,32,256]{3,2,0,1:T(8,128)(2,1)S(1)}, u32[]{:S(2)}, u32[]{:S(2)}) collective-permute-start(bf16[2,5,32,256]{3,2,0,1:T(8,128)(2,1)S(1)} %get-tuple-element.50), channel_id=1, source_target_pairs={{0,8},{8,16},{16,24},{24,32},{32,40},{40,48},{48,56},{56,64},{64,7... | collective-permute-start | bytes 491528 | tf_op jit(solution)/shard_map/ppermute | solution.py:33
  119.4 6.6 %collective-permute-start.3 = (bf16[2,5,32,256]{3,2,0,1:T(8,128)(2,1)S(1)}, bf16[2,5,32,256]{3,2,0,1:T(8,128)(2,1)S(1)}, u32[]{:S(2)}, u32[]{:S(2)}) collective-permute-start(bf16[2,5,32,256]{3,2,0,1:T(8,128)(2,1)S(1)} %get-tuple-element.51), channel_id=1, source_target_pairs={{8,0},{16,8},{24,16},{32,24},{40,32},{48,40},{56,48},{64,56},{72,6... | collective-permute-start | bytes 491528 | tf_op jit(solution)/shard_map/ppermute | solution.py:35
  127.0 192.7 %reduce-scatter.3.cloned.1.call-start = ((), (), s32[]{:S(2)}) async-start(), calls=%async_computation.5 | async-start | bytes 2949120 | tf_op jit(solution)/shard_map/reduce_scatter | solution.py:64
  210.8 2.5 copy-start.1
  240.5 9.4 %copy-start.4 = (s32[2]{0:T(128)S(1)}, s32[2]{0:T(128)}, u32[]{:S(2)}) copy-start(s32[2]{0:T(128)} %param.8) | copy-start | bytes 28
  240.5 15.3 %copy-start.3 = (f32[2,4096]{1,0:T(2,128)S(1)}, f32[2,4096]{1,0:T(2,128)}, u32[]{:S(2)}) copy-start(f32[2,4096]{1,0:T(2,128)} %param.11) | copy-start | bytes 98308
  240.7 1.2 copy-start.2
  241.9 20.2 %slice-start = ((s8[6291456]{0:T(1024)(128)(4,1)}), s8[2097152]{0:T(1024)(128)(4,1)S(1)}, s32[]{:S(2)}) async-start(s8[6291456]{0:T(1024)(128)(4,1)} %bitcast.196), calls=%async_computation.7 | async-start | bytes 4194304
  242.8 13.5 %collective-permute-start.4 = (bf16[1,3,256,256]{3,2,1,0:T(8,128)(2,1)}, bf16[1,3,256,256]{3,2,1,0:T(8,128)(2,1)S(1)}, u32[]{:S(2)}, u32[]{:S(2)}) collective-permute-start(bf16[1,3,256,256]{3,2,1,0:T(8,128)(2,1)} %bitcast.45), channel_id=1, source_target_pairs={{0,8},{8,16},{16,24},{24,32},{32,40},{40,48},{48,56},{56,64},{64,7... | collective-permute-start | bytes 1179656 | tf_op jit(solution)/shard_map/ppermute | solution.py:33
  247.8 9.4 %collective-permute-start.5 = (bf16[1,3,256,256]{3,2,1,0:T(8,128)(2,1)}, bf16[1,3,256,256]{3,2,1,0:T(8,128)(2,1)}, u32[]{:S(2)}, u32[]{:S(2)}) collective-permute-start(bf16[1,3,256,256]{3,2,1,0:T(8,128)(2,1)} %bitcast.47), channel_id=1, source_target_pairs={{8,0},{16,8},{24,16},{32,24},{40,32},{48,40},{56,48},{64,56},{72,6... | collective-permute-start | bytes 1179656 | tf_op jit(solution)/shard_map/ppermute | solution.py:35
  257.3 4.9 %slice-start.1 = ((s8[6291456]{0:T(1024)(128)(4,1)}), s8[4194304]{0:T(1024)(128)(4,1)S(1)}, s32[]{:S(2)}) async-start(s8[6291456]{0:T(1024)(128)(4,1)} %bitcast.196), calls=%async_computation.8 | async-start | bytes 8388608
  288.9 52.1 %reduce-scatter.5.cloned.1.call-start = ((), (), s32[]{:S(2)}) async-start(), calls=%async_computation.6 | async-start | bytes 884736 | tf_op jit(solution)/shard_map/reduce_scatter | solution.py:64
  341.9 8.6 %collective-permute-start.6 = (bf16[3,32,256]{2,1,0:T(8,128)(2,1)S(1)}, bf16[3,32,256]{2,1,0:T(8,128)(2,1)S(1)}, u32[]{:S(2)}, u32[]{:S(2)}) collective-permute-start(bf16[3,32,256]{2,1,0:T(8,128)(2,1)S(1)} %get-tuple-element.54), channel_id=1, source_target_pairs={{0,8},{8,16},{16,24},{24,32},{32,40},{40,48},{48,56},{56,64},{64,7... | collective-permute-start | bytes 147464 | tf_op jit(solution)/shard_map/ppermute | solution.py:22
  347.6 5.4 %collective-permute-start.7 = (bf16[3,32,256]{2,1,0:T(8,128)(2,1)S(1)}, bf16[3,32,256]{2,1,0:T(8,128)(2,1)S(1)}, u32[]{:S(2)}, u32[]{:S(2)}) collective-permute-start(bf16[3,32,256]{2,1,0:T(8,128)(2,1)S(1)} %get-tuple-element.55), channel_id=1, source_target_pairs={{8,0},{16,8},{24,16},{32,24},{40,32},{48,40},{56,48},{64,56},{72,6... | collective-permute-start | bytes 147464 | tf_op jit(solution)/shard_map/ppermute | solution.py:22
Sparse Core Ops, SparseCore 0:
  21.3 82.8 all-gather.2
  127.1 78.2 all-gather.4
  289.1 30.5 reduce-scatter.2
  321.9 19.1 reduce-scatter.4

commit v2 on v1

--- a/solution.py
+++ b/solution.py
@@ -3,12 +3,11 @@
 from jax import lax
 from jax.experimental import pallas as pl
 from jax.experimental.pallas import tpu as pltpu
-from jax.sharding import Mesh
 from jax.sharding import PartitionSpec as P
 
 ITERS = 2
-COL = ("col_0", "col_1")
-ROW_COL = ("row", "col_0", "col_1")
+COL = "col"
+ROW_COL = ("row", "col")
 
 
 slater_cx = 0.7386
@@ -180,18 +179,350 @@
     return jnp.swapaxes(density, 2, 3).reshape(tiles, points), terms
 
 
-def band_product(left, right_padded):
-    blocks = left.shape[0]
-    total = None
-    for offset_step in range(5):
-        shifted = right_padded[offset_step : offset_step + blocks]
-        widened = jnp.pad(shifted, ((0, 0), (2, 2), (0, 0), (0, 0)))
-        picked = widened[:, 4 - offset_step : 9 - offset_step]
-        term = jnp.einsum(
-            "brk,bdkc->bdrc", left[:, offset_step], picked, preferred_element_type=jnp.float32
+BLOCKS = 64
+BAND = 5
+HALF = 128
+WIDTH = 256
+SLICE = 32
+COLS = 8
+FIRST_PIECES = {
+    -2: ((2, 2, 0),),
+    -1: ((2, 1, 2), (4, 1, 3)),
+    0: ((0, 5, 4),),
+    1: ((2, 2, 9),),
+    2: ((2, 1, 11),),
+}
+FIRST_ROLE = {-2: (0, 2), -1: (2, 2), 0: (4, 5), 1: (9, 2), 2: (11, 1)}
+FIRST_SLOT = {(-2, -2): 0, (-2, -1): 1, (-1, -1): 2, (-1, 1): 3, (1, 1): 9, (1, 2): 10, (2, 2): 11}
+SECOND_ROLE = {-2: (0, 3, 2), -1: (3, 4, 1), 0: (7, 5, 0), 1: (12, 4, 0), 2: (16, 3, 0)}
+
+
+def first_block(a, b):
+    if a == 0:
+        return 6 + b, False
+    if b == 0:
+        return 6 + a, True
+    if (a, b) in FIRST_SLOT:
+        return FIRST_SLOT[a, b], False
+    return FIRST_SLOT[b, a], True
+
+
+def second_block(a, b):
+    return SECOND_ROLE[a][0] + b - max(-2, a - 2), False
+
+
+def product(left, right, where):
+    columns = []
+    for b in range(-2, 3):
+        total = None
+        for a in range(max(-2, b - 2), min(2, b + 2) + 1):
+            slot, flipped = where(a, b)
+            term = lax.dot_general(
+                left(a + 2),
+                right[slot],
+                (((1,), (1 if flipped else 0,)), ((), ())),
+                preferred_element_type=jnp.float32,
+            )
+            total = term if total is None else total + term
+        columns.append(total)
+    return columns
+
+
+def purify_kernel(
+    density,
+    kept,
+    purified,
+    first,
+    second,
+    squares,
+    mine,
+    final,
+    kept_other,
+    send_first,
+    recv_first,
+    send_pass,
+    recv_pass,
+    send_second,
+    recv_second,
+    send_pass_second,
+    recv_pass_second,
+    send_out,
+    recv_out,
+    kept_sems,
+    own_sem,
+):
+    q = lax.axis_index("row")
+    c = lax.axis_index("col")
+    m = q // 2
+    h = q % 2
+    i = 8 * m + c
+    rows = pl.ds(pl.multiple_of(HALF * h, HALF), HALF)
+    sibling = dict(device_id={"row": 2 * m + 1 - h, "col": c}, device_id_type=pl.DeviceIdType.MESH)
+
+    def chip(block_row):
+        return dict(
+            device_id={"row": 2 * (block_row // 8) + h, "col": block_row % 8},
+            device_id_type=pl.DeviceIdType.MESH,
         )
-        total = term if total is None else total + term
-    return total
+
+    barrier = pltpu.get_barrier_semaphore()
+
+    def greet(row, col):
+        pl.semaphore_signal(
+            barrier, inc=1, device_id={"row": row, "col": col}, device_id_type=pl.DeviceIdType.MESH
+        )
+
+    @pl.loop(0, COLS)
+    def _(other):
+        greet(2 * m + 1 - h, other)
+
+        @pl.when(other != c)
+        def _():
+            greet(q, other)
+
+        @pl.when((m > 0) & (((h == 0) & (other >= 6)) | ((h == 1) & (c <= 1))))
+        def _():
+            greet(q - 2, other)
+
+        @pl.when((m < 7) & (((h == 1) & (other <= 1)) | ((h == 0) & (c >= 6))))
+        def _():
+            greet(q + 2, other)
+
+    lower = jnp.where(m > 0, jnp.where(h == 0, 2, jnp.where(c <= 1, 8, 0)), 0)
+    upper = jnp.where(m < 7, jnp.where(h == 1, 2, jnp.where(c >= 6, 8, 0)), 0)
+    pl.semaphore_wait(barrier, 15 + lower + upper)
+
+    kept_copy = pltpu.make_async_remote_copy(
+        kept, kept_other, kept_sems.at[0], kept_sems.at[1], **sibling
+    )
+    kept_copy.start()
+
+    def first_copies(local, act):
+        k = 4 * q + local
+        place = pl.ds(pl.multiple_of(SLICE * c, SLICE), SLICE)
+        index = 0
+        for role, pieces in FIRST_PIECES.items():
+            target = k - role
+            valid = (target >= 0) & (target < BLOCKS)
+            for diagonal, count, slot in pieces:
+                source = density.at[local, pl.ds(diagonal, count)]
+                landing = first.at[pl.ds(slot, count), place]
+
+                @pl.when(valid & (target != i))
+                def _():
+                    act(
+                        pltpu.make_async_remote_copy(
+                            source,
+                            landing,
+                            send_first.at[local, index],
+                            recv_first.at[role + 2],
+                            **chip(target),
+                        ),
+                        True,
+                    )
+
+                @pl.when(target == i)
+                def _():
+                    act(pltpu.make_async_copy(source, landing, recv_first.at[role + 2]), False)
+
+                index += 1
+
+    @pl.loop(0, 4)
+    def _(local):
+        first_copies(local, lambda copy, remote: copy.start())
+
+    def pass_on(role):
+        slot, count = FIRST_ROLE[role]
+        part = first.at[pl.ds(slot, count)]
+        return pltpu.make_async_remote_copy(
+            part, part, send_pass.at[role + 2], recv_pass.at[role + 2], **sibling
+        )
+
+    order = (0, -1, 1, -2, 2)
+    for role in order:
+        slot, count = FIRST_ROLE[role]
+        part = first.at[pl.ds(slot, count)]
+        k = i + role
+        valid = (k >= 0) & (k < BLOCKS)
+
+        @pl.when(valid & ((k // 4) % 2 == h))
+        def _():
+            pltpu.make_async_copy(part, part, recv_first.at[role + 2]).wait()
+            pass_on(role).start()
+
+        @pl.when(jnp.logical_not(valid))
+        def _():
+            first[pl.ds(slot, count)] = jnp.zeros((count, WIDTH, WIDTH), jnp.bfloat16)
+            start, number, _ = SECOND_ROLE[role]
+            second[pl.ds(start, number)] = jnp.zeros((number, WIDTH, WIDTH), jnp.bfloat16)
+
+    for role in order:
+        k = i + role
+
+        @pl.when((k >= 0) & (k < BLOCKS) & ((k // 4) % 2 != h))
+        def _():
+            pass_on(role).wait_recv()
+
+    kept_copy.wait()
+    near_kept = kept[c % 4]
+    far_kept = kept_other[c % 4]
+    mask = jnp.where(h == c // 4, near_kept, far_kept)
+
+    def iterate(left, right, where, result):
+        for d, total in enumerate(product(left, right, where)):
+            squares[d] = jnp.where(mask[d : d + 1] > 0, total, 0.0).astype(jnp.bfloat16)
+        for d, total in enumerate(product(lambda a: squares[a], right, where)):
+            value = 3.0 * squares[d].astype(jnp.float32) - 2.0 * total
+            result[d] = jnp.where(mask[d : d + 1] > 0, value, 0.0).astype(jnp.bfloat16)
+
+    iterate(lambda a: first[4 + a, rows, :], first, first_block, mine)
+
+    own = pltpu.make_async_copy(mine, second.at[pl.ds(7, 5), rows], own_sem)
+    own.start()
+    own_far = pltpu.make_async_remote_copy(
+        mine, second.at[pl.ds(7, 5), rows], send_pass_second.at[2], recv_pass_second.at[2], **sibling
+    )
+    own_far.start()
+
+    def second_copy(role):
+        start, number, diagonal = SECOND_ROLE[role]
+        return pltpu.make_async_remote_copy(
+            mine.at[pl.ds(diagonal, number)],
+            second.at[pl.ds(start, number), rows],
+            send_second.at[role + 2],
+            recv_second.at[role + 2],
+            **chip(i - role),
+        )
+
+    def second_pass(role):
+        start, number, _ = SECOND_ROLE[role]
+        part = second.at[pl.ds(start, number), rows]
+        return pltpu.make_async_remote_copy(
+            part, part, send_pass_second.at[role + 2], recv_pass_second.at[role + 2], **sibling
+        )
+
+    others = (-2, 2, -1, 1)
+    for role in others:
+        target = i - role
+
+        @pl.when((target >= 0) & (target < BLOCKS))
+        def _():
+            second_copy(role).start()
+
+    for role in (-1, 1, -2, 2):
+        k = i + role
+
+        @pl.when((k >= 0) & (k < BLOCKS))
+        def _():
+            second_copy(role).wait_recv()
+            second_pass(role).start()
+
+    for role in (-1, 1, -2, 2):
+        k = i + role
+
+        @pl.when((k >= 0) & (k < BLOCKS))
+        def _():
+            second_pass(role).wait_recv()
+
+    own.wait()
+    own_far.wait_recv()
+    iterate(lambda a: mine[a], second, second_block, final)
+
+    def out_copies(act):
+        for u in range(4):
+            source = final.at[:, pl.ds(SLICE * u, SLICE)]
+            landing = purified.at[c % 4]
+            row, col = 2 * m + c // 4, 4 * h + u
+            here = (row == q) & (col == c)
+
+            @pl.when(jnp.logical_not(here))
+            def _():
+                act(
+                    pltpu.make_async_remote_copy(
+                        source,
+                        landing,
+                        send_out.at[u],
+                        recv_out.at[c % 4],
+                        device_id={"row": row, "col": col},
+                        device_id_type=pl.DeviceIdType.MESH,
+                    ),
+                    True,
+                )
+
+            @pl.when(here)
+            def _():
+                act(pltpu.make_async_copy(source, landing, recv_out.at[c % 4]), False)
+
+    out_copies(lambda copy, remote: copy.start())
+
+    @pl.loop(0, 4)
+    def _(local):
+        first_copies(local, lambda copy, remote: copy.wait_send() if remote else None)
+
+    for role in order:
+        k = i + role
+
+        @pl.when((k >= 0) & (k < BLOCKS) & ((k // 4) % 2 == h))
+        def _():
+            pass_on(role).wait_send()
+
+    own_far.wait_send()
+    for role in (-1, 1, -2, 2):
+        target = i - role
+
+        @pl.when((target >= 0) & (target < BLOCKS))
+        def _():
+            second_copy(role).wait_send()
+
+        k = i + role
+
+        @pl.when((k >= 0) & (k < BLOCKS))
+        def _():
+            second_pass(role).wait_send()
+
+    out_copies(lambda copy, remote: copy.wait_send() if remote else None)
+    for local in range(4):
+        part = purified.at[local]
+        pltpu.make_async_copy(part, part, recv_out.at[local]).wait()
+
+
+def purify(density, pattern):
+    blocks, diagonals, width, across = density.shape
+    kept = jnp.broadcast_to(
+        jnp.pad((pattern > 0).astype(jnp.float32), ((0, 0), (0, 3)))[:, :, None], (blocks, 8, WIDTH)
+    )
+    bf16, dma = jnp.bfloat16, pltpu.SemaphoreType.DMA
+    vmem = pl.BlockSpec(memory_space=pltpu.VMEM)
+    return pl.pallas_call(
+        purify_kernel,
+        name="purify",
+        in_specs=[vmem, vmem],
+        out_specs=vmem,
+        out_shape=jax.ShapeDtypeStruct(density.shape, bf16),
+        scratch_shapes=[
+            pltpu.VMEM((12, WIDTH, WIDTH), bf16),
+            pltpu.VMEM((19, WIDTH, WIDTH), bf16),
+            pltpu.VMEM((BAND, HALF, WIDTH), bf16),
+            pltpu.VMEM((BAND, HALF, WIDTH), bf16),
+            pltpu.VMEM((BAND, HALF, WIDTH), bf16),
+            pltpu.VMEM((4, 8, WIDTH), jnp.float32),
+            dma((4, 6)),
+            dma((5,)),
+            dma((5,)),
+            dma((5,)),
+            dma((5,)),
+            dma((5,)),
+            dma((5,)),
+            dma((5,)),
+            dma((4,)),
+            dma((4,)),
+            dma((2,)),
+            dma(()),
+        ],
+        compiler_params=pltpu.CompilerParams(
+            collective_id=0, has_side_effects=True, vmem_limit_bytes=40 * 1024 * 1024
+        ),
+    )(density, kept)
 
 
 def window_of(band_three, lead, offset, functions):
@@ -237,14 +568,7 @@
     step_size = functions // 3
     kept = (pattern > 0)[:, :, None, None]
     current = jnp.where(kept, density, jnp.zeros_like(density))
-    for iteration in range(ITERS):
-        near_right = padded(current, (("row", 0),), 2)
-        right_full = lax.all_gather(near_right, COL, axis=2, tiled=True)
-        square = jnp.where(kept, band_product(current, right_full), 0.0).astype(jnp.bfloat16)
-        cubic = band_product(square, right_full)
-        current = jnp.where(kept, 3.0 * square.astype(jnp.float32) - 2.0 * cubic, 0.0).astype(
-            jnp.bfloat16
-        )
+    current = purify(current, pattern)
     rows_band = gather_directly(current[:, 1:4], COL, 2)
     near = padded(rows_band, (("row", 0),), 1)
     tiles_here = windows.shape[0]
@@ -258,14 +582,13 @@
     local_terms = jnp.zeros((band_rows + 2, 3, block_size, block_size), jnp.float32)
     for t in range(tiles_here):
         local_terms = spread_term(local_terms, contributions[t], leads[t], offsets[t])
-    owner_part = scatter_axes(local_terms.astype(jnp.bfloat16), COL, (1, 0), 2).astype(jnp.float32)
+    owner_part = scatter_axes(local_terms.astype(jnp.bfloat16), (COL,), (0,), 2).astype(jnp.float32)
     mine = edge_rows(owner_part)
     xc_matrix = jnp.where(kept, jnp.pad(mine, ((0, 0), (1, 1), (0, 0), (0, 0))), 0.0)
     return (current, xc_matrix, densities)
 
 
 def solution(mesh):
-    torus = Mesh(mesh.devices.reshape(mesh.shape["row"], 2, 4), ("row", "col_0", "col_1"))
     placed = (
         P("row", None, COL, None),
         P("row", None),
@@ -276,7 +599,7 @@
     )
     return jax.shard_map(
         on_device,
-        mesh=torus,
+        mesh=mesh,
         in_specs=placed,
         out_specs=(P("row", None, COL, None), P("row", None, COL, None), P(ROW_COL, None)),
         check_vma=False,

time: 362 us -> 227 us (0.63)
  waiting for transfers between devices: 226 us -> 74.8 us
  Pallas kernels: 22.8 us -> 70.7 us
  local copies, waits for them, and re-layouts: 22.4 us -> 10.4 us
  starting transfers between devices: 25.8 us -> 14.3 us
  matrix products: 9.05 us -> 0 us
    all_gather x2 -> x0, waiting for transfers between devices: 161 us -> none  [on_device(): right_full = lax.all_gather(near_right, COL, axis=2, tiled=True)]
    pallas_call x0 -> x1, Pallas kernels: none -> 48 us  [purify(): pl.pallas_call(purify_kernel, name='purify', in_specs=[vmem, vmem], out_s...]
    reduce_scatter x2 -> x1, waiting for transfers between devices: 52 us -> 72.3 us  [sum_in_order(): pieces = lax.psum_scatter(pieces, axes[k], scatter_dimension=0, tiled=True)]
    ppermute x3 -> x1, starting transfers between devices: 13.9 us -> 3.17 us  [padded(): lax.ppermute(tail, axis, [(i, (i + 1) % count) for i in range(ends)])]
    ppermute x3 -> x1, waiting for transfers between devices: 9.78 us -> 0.01 us  [padded(): lax.ppermute(head, axis, [((i + 1) % count, i) for i in range(ends)])]
    dot_general x20 -> x0, matrix products: 9.05 us -> none  [band_product(): jnp.einsum('brk,bdkc->bdrc', left[:, offset_step], picked, preferred_elem...]
    slice x2 -> x1, local copies, waits for them, and re-layouts: 8.97 us -> 0.01 us  [edge_rows(): own_rows[1:blocks - 1]]
    unnamed x16 -> x9, local copies, waits for them, and re-layouts: 6.16 us -> 0.74 us
  transfers between devices with their start and end apart: 12 -> 5, of which waited for: 10 -> 2; matrix products, arithmetic and copies ran while one was open for 1% -> 1% of each run, Pallas kernels for 0% -> 0%
where the time goes in v2:
time: 227 us; the launch traced here: 226 us
  waiting for transfers between devices  74.8 us (33%)
  Pallas kernels  70.7 us (31%)
  blocking collectives  27 us (12%)
  between operations  19.6 us (9%)
  starting transfers between devices  14.3 us (6%)
  local copies, waits for them, and re-layouts  10.4 us (5%)
  other arithmetic  9.54 us (4%)
    reduce_scatter x1, waiting for transfers between devices, sum_in_order(): pieces = lax.psum_scatter(pieces, axes[k], scatter_dimension=0, tiled=True)  72.3 us
    pallas_call x1, Pallas kernels, purify(): pl.pallas_call(purify_kernel, name='purify', in_specs=[vmem, vmem], out_s...  48 us
    all_to_all x1, blocking collectives, sent_to_all(): lax.all_to_all(jnp.broadcast_to(value[None], (length, *value.shape)), axi...  27 us
    pallas_call x1, Pallas kernels, tile_terms(): pl.pallas_call(tile_kernel, name='tile_terms', grid=(tiles, steps), in_sp...  22.8 us
    ppermute x2, starting transfers between devices, shifted_2(): return lax.ppermute(value, axis, pairs)  7.11 us
  transfers between devices with their start and end apart: 5, of which 2 were waited for; matrix products, arithmetic and copies ran while one was open for 1% of the time, Pallas kernels for 0%

profile of v2, /device:TPU:1, one launch (start us, length us, event | category | flops | bytes accessed | tf_op | source)
XLA Modules:
  0.0 226.3 jit_solution(14316587539878977404)
XLA Ops:
  7.2 0.0 reduce-scatter.2.cloned.1.call-start
  7.2 0.7 broadcast_compare_fusion
  7.9 1.1 broadcast_select_fusion.density
  9.0 0.1 broadcast_in_dim.51.kept
  9.0 48.0 %purify.1 = bf16[4,5,32,256]{3,2,1,0:T(8,128)(2,1)S(1)} custom-call(bf16[4,5,32,256]{3,2,1,0:T(8,128)(2,1)S(1)} %broadcast_select_fusion.density, f32[4,8,256]{2,1,0:T(8,128)S(1)} %broadcast_in_dim.51.kept), custom_call_target="tpu_custom_call" | custom-call | tf_op jit(solution)/shard_map/purify/pallas_call | solution.py:496
  57.0 0.2 broadcast_in_dim.53
  57.2 27.0 %all_to_all.5 = bf16[8,4,3,32,256]{4,3,2,1,0:T(8,128)(2,1)S(1)} all-to-all(bf16[8,4,3,32,256]{4,3,2,1,0:T(8,128)(2,1)S(1)} %broadcast_in_dim.53), channel_id=1, replica_groups=mesh['row'=16,'col'=8] {'col'}, dimensions={0} | all-to-all | bytes 3145728 | tf_op jit(solution)/shard_map/all_to_all | solution.py:49
  84.2 0.0 copy-start.1
  84.2 0.0 copy-start
  84.2 1.3 copy.23
  85.5 0.0 slice-start
  85.5 2.2 fusion.19
  87.8 4.0 %collective-permute-start.1 = (bf16[1,3,256,256]{3,2,1,0:T(8,128)(2,1)}, bf16[1,3,256,256]{3,2,1,0:T(8,128)(2,1)S(1)}, u32[]{:S(2)}, u32[]{:S(2)}) collective-permute-start(bf16[1,3,256,256]{3,2,1,0:T(8,128)(2,1)} %bitcast.3), channel_id=1, source_target_pairs={{8,0},{16,8},{24,16},{32,24},{40,32},{48,40},{56,48},{64,56},{72,6... | collective-permute-start | bytes 1179656 | tf_op jit(solution)/shard_map/ppermute | solution.py:34
  91.8 3.2 %collective-permute-start = (bf16[1,3,256,256]{3,2,1,0:T(8,128)(2,1)}, bf16[1,3,256,256]{3,2,1,0:T(8,128)(2,1)}, u32[]{:S(2)}, u32[]{:S(2)}) collective-permute-start(bf16[1,3,256,256]{3,2,1,0:T(8,128)(2,1)} %bitcast.1), channel_id=1, source_target_pairs={{0,8},{8,16},{16,24},{24,32},{32,40},{40,48},{48,56},{56,64},{64,7... | collective-permute-start | bytes 1179656 | tf_op jit(solution)/shard_map/ppermute | solution.py:32
  94.9 0.0 copy-done.1
  95.0 0.6 fusion.21
  100.8 0.0 copy-done
  100.8 0.3 reshape.36
  101.1 0.2 copy.16
  101.3 0.0 collective-permute-done.1
  101.3 0.0 collective-permute-done
  101.3 0.0 slice-start.1
  101.3 1.9 pad_maximum_fusion
  103.2 0.1 dynamic-slice_bitcast_fusion.4
  103.3 2.7 %fusion.11 = (bf16[1,384,384]{2,1,0:T(8,128)(2,1)S(1)}, bf16[1,384,384]{2,1,0:T(8,128)(2,1)S(1)}) fusion(s32[]{:T(128)S(6)} %select_n.55, bf16[256,256]{1,0:T(8,128)(2,1)S(1)} %get-tuple-element.10, bf16[256,256]{1,0:T(8,128)(2,1)S(1)} %get-tuple-element.9, bf16[256,256]{1,0:T(8,128)(2,1)S(1)} %get-tuple-element.8, ...), kind=kLoop, calls=%fused_computation.35 | loop fusion | flops 2359296 | bytes 1638408 | tf_op jit(solution)/shard_map/stack | solution.py:578
  106.0 0.1 pad_maximum_fusion.5.window_ref
  106.1 0.0 slice-done
  106.1 0.0 slice-done.1
  106.1 22.8 %tile_terms.1 = (f32[2,4,8,128]{3,2,1,0:T(8,128)S(1)}, f32[2,384,384]{2,1,0:T(8,128)S(1)}) custom-call(bf16[2,384,384]{2,1,0:T(8,128)(2,1)S(1)} %pad_maximum_fusion.5.window_ref, bf16[2,4096,384]{2,1,0:T(8,128)(2,1)S(1)} %bitcast.85, bf16[3,2,4096,384]{3,2,1,0:T(8,128)(2,1)} %grads_ref.1, f32[2,4,8,128]{3,2,1,0:T(8,128)S(1)} %bitcast.86), custom_call_target="tpu_custom_call" | custom-call | flops 4831838208 | bytes 25165824 | tf_op jit(solution)/shard_map/tile_terms/pallas_call | solution.py:147
  128.9 0.1 broadcast.22.clone
  129.0 0.1 bitcast_dynamic-update-slice_fusion
  129.1 0.1 broadcast.22.clone.1
  129.2 0.1 bitcast_dynamic-update-slice_fusion.1
  129.3 0.1 slice_bitcast_fusion.7
  129.4 0.1 slice_bitcast_fusion.3
  129.5 0.3 fusion.6
  129.9 0.5 broadcast_in_dim.52
  130.3 0.1 maximum_dynamic-update-slice_fusion
  130.5 0.4 fusion
  130.9 0.3 convert_element_type.24
  131.2 1.7 copy.22
  132.9 0.0 reduce-scatter.2.cloned.1.call-update
  132.9 0.2 copy.18
  133.1 0.9 reshape.38
  134.0 72.3 %reduce-scatter.2.cloned.1.call-done = bf16[1,6,3,32,256]{4,3,2,1,0:T(8,128)(2,1)} async-done(((bf16[8,6,3,32,256]{4,3,2,1,0:T(8,128)(2,1)}), bf16[1,6,3,32,256]{4,3,2,1,0:T(8,128)(2,1)}) %reduce-scatter.2.cloned.1.call-update) | async-done | bytes 294928 | tf_op jit(solution)/shard_map/reduce_scatter | solution.py:63
  206.4 0.8 slice_bitcast_fusion.12
  207.2 5.2 %collective-permute-start.2 = (bf16[3,32,256]{2,1,0:T(8,128)(2,1)S(1)}, bf16[3,32,256]{2,1,0:T(8,128)(2,1)S(1)}, u32[]{:S(2)}, u32[]{:S(2)}) collective-permute-start(bf16[3,32,256]{2,1,0:T(8,128)(2,1)S(1)} %get-tuple-element.29), channel_id=1, source_target_pairs={{0,8},{8,16},{16,24},{24,32},{32,40},{40,48},{48,56},{56,64},{64,7... | collective-permute-start | bytes 147464 | tf_op jit(solution)/shard_map/ppermute | solution.py:21
  212.4 1.9 collective-permute-start.3
  214.3 1.0 convert_element_type.25
  215.4 0.0 collective-permute-done.2
  215.4 2.4 %collective-permute-done.3 = bf16[3,32,256]{2,1,0:T(8,128)(2,1)S(1)} collective-permute-done((bf16[3,32,256]{2,1,0:T(8,128)(2,1)S(1)}, bf16[3,32,256]{2,1,0:T(8,128)(2,1)S(1)}, u32[]{:S(2)}, u32[]{:S(2)}) %collective-permute-start.3) | collective-permute-done | bytes 49184 | tf_op jit(solution)/shard_map/ppermute | solution.py:21
  217.8 0.9 fusion.7
  218.8 0.7 copy.29
  (6 shorter events, 0.1 us)
Async XLA Ops:
  7.2 199.2 %reduce-scatter.2.cloned.1.call-start = ((), (), s32[]{:S(2)}) async-start(), calls=%async_computation.2 | async-start | bytes 2654208 | tf_op jit(solution)/shard_map/reduce_scatter | solution.py:63
  84.2 10.7 %copy-start.1 = (s32[2]{0:T(128)S(1)}, s32[2]{0:T(128)}, u32[]{:S(2)}) copy-start(s32[2]{0:T(128)} %param.8) | copy-start | bytes 28
  84.2 16.6 %copy-start = (f32[2,4096]{1,0:T(2,128)S(1)}, f32[2,4096]{1,0:T(2,128)}, u32[]{:S(2)}) copy-start(f32[2,4096]{1,0:T(2,128)} %param.11) | copy-start | bytes 98308
  85.5 20.5 %slice-start = ((s8[6291456]{0:T(1024)(128)(4,1)}), s8[2097152]{0:T(1024)(128)(4,1)S(1)}, s32[]{:S(2)}) async-start(s8[6291456]{0:T(1024)(128)(4,1)} %bitcast.84), calls=%async_computation.3 | async-start | bytes 4194304
  87.8 13.5 %collective-permute-start.1 = (bf16[1,3,256,256]{3,2,1,0:T(8,128)(2,1)}, bf16[1,3,256,256]{3,2,1,0:T(8,128)(2,1)S(1)}, u32[]{:S(2)}, u32[]{:S(2)}) collective-permute-start(bf16[1,3,256,256]{3,2,1,0:T(8,128)(2,1)} %bitcast.3), channel_id=1, source_target_pairs={{8,0},{16,8},{24,16},{32,24},{40,32},{48,40},{56,48},{64,56},{72,6... | collective-permute-start | bytes 1179656 | tf_op jit(solution)/shard_map/ppermute | solution.py:34
  91.8 9.5 %collective-permute-start = (bf16[1,3,256,256]{3,2,1,0:T(8,128)(2,1)}, bf16[1,3,256,256]{3,2,1,0:T(8,128)(2,1)}, u32[]{:S(2)}, u32[]{:S(2)}) collective-permute-start(bf16[1,3,256,256]{3,2,1,0:T(8,128)(2,1)} %bitcast.1), channel_id=1, source_target_pairs={{0,8},{8,16},{16,24},{24,32},{32,40},{40,48},{48,56},{56,64},{64,7... | collective-permute-start | bytes 1179656 | tf_op jit(solution)/shard_map/ppermute | solution.py:32
  101.3 4.8 %slice-start.1 = ((s8[6291456]{0:T(1024)(128)(4,1)}), s8[4194304]{0:T(1024)(128)(4,1)S(1)}, s32[]{:S(2)}) async-start(s8[6291456]{0:T(1024)(128)(4,1)} %bitcast.84), calls=%async_computation.4 | async-start | bytes 8388608
  207.2 8.2 %collective-permute-start.2 = (bf16[3,32,256]{2,1,0:T(8,128)(2,1)S(1)}, bf16[3,32,256]{2,1,0:T(8,128)(2,1)S(1)}, u32[]{:S(2)}, u32[]{:S(2)}) collective-permute-start(bf16[3,32,256]{2,1,0:T(8,128)(2,1)S(1)} %get-tuple-element.29), channel_id=1, source_target_pairs={{0,8},{8,16},{16,24},{24,32},{32,40},{40,48},{48,56},{56,64},{64,7... | collective-permute-start | bytes 147464 | tf_op jit(solution)/shard_map/ppermute | solution.py:21
  212.4 5.4 %collective-permute-start.3 = (bf16[3,32,256]{2,1,0:T(8,128)(2,1)S(1)}, bf16[3,32,256]{2,1,0:T(8,128)(2,1)S(1)}, u32[]{:S(2)}, u32[]{:S(2)}) collective-permute-start(bf16[3,32,256]{2,1,0:T(8,128)(2,1)S(1)} %get-tuple-element.30), channel_id=1, source_target_pairs={{8,0},{16,8},{24,16},{32,24},{40,32},{48,40},{56,48},{64,56},{72,6... | collective-permute-start | bytes 147464 | tf_op jit(solution)/shard_map/ppermute | solution.py:21
Sparse Core Ops, SparseCore 0:
  133.0 73.2 reduce-scatter.1

commit v3 on v2

--- a/solution.py
+++ b/solution.py
@@ -5,7 +5,6 @@
 from jax.experimental.pallas import tpu as pltpu
 from jax.sharding import PartitionSpec as P
 
-ITERS = 2
 COL = "col"
 ROW_COL = ("row", "col")
 
@@ -13,65 +12,6 @@
 slater_cx = 0.7386
 kappa_pbe = 0.804
 mu_pbe = 0.2195
-
-
-def shifted_2(value, axis, by):
-    length = lax.axis_size(axis)
-    pairs = [(i, i + by) for i in range(length) if 0 <= i + by < length]
-    return lax.ppermute(value, axis, pairs)
-
-
-def padded(cells, sides, width):
-    for axis, dim in sides:
-        count = lax.axis_size(axis)
-        ends = count - 1
-        head = lax.slice_in_dim(cells, 0, width, axis=dim)
-        tail = lax.slice_in_dim(cells, cells.shape[dim] - width, cells.shape[dim], axis=dim)
-        cells = jnp.concatenate(
-            [
-                lax.ppermute(tail, axis, [(i, (i + 1) % count) for i in range(ends)]),
-                cells,
-                lax.ppermute(head, axis, [((i + 1) % count, i) for i in range(ends)]),
-            ],
-            axis=dim,
-        )
-    return cells
-
-
-def in_order(pieces, dim):
-    pieces = jnp.moveaxis(pieces, 0, dim)
-    lengths = pieces.shape
-    return pieces.reshape(*lengths[:dim], lengths[dim] * lengths[dim + 1], *lengths[dim + 2 :])
-
-
-def sent_to_all(value, axis):
-    length = lax.axis_size(axis)
-    return lax.all_to_all(
-        jnp.broadcast_to(value[None], (length, *value.shape)), axis, 0, 0, tiled=True
-    )
-
-
-def gather_directly(value, axis, dim):
-    return in_order(sent_to_all(value, axis), dim)
-
-
-def sum_in_order(pieces, axes, sequence):
-    inside = pieces.shape[1:]
-    pieces = pieces.reshape(*(lax.axis_size(a) for a in axes), *inside)
-    pieces = jnp.moveaxis(pieces, sequence, range(len(axes))).reshape(-1, *inside)
-    for k in sequence:
-        pieces = lax.psum_scatter(pieces, axes[k], scatter_dimension=0, tiled=True)
-    return pieces[0]
-
-
-def cut_along(value, dim, length):
-    before, after = (value.shape[:dim], value.shape[dim + 1 :])
-    return jnp.moveaxis(value.reshape(*before, length, -1, *after), dim, 0)
-
-
-def scatter_axes(value, axes, sequence, dim):
-    length = lax.axis_size(axes)
-    return sum_in_order(cut_along(value, dim, length), axes, sequence)
 
 
 POINT_BLOCK = 1024
@@ -90,7 +30,9 @@
     return by_density, by_gradient
 
 
-def tile_kernel(window_ref, values_ref, grads_ref, weights_ref, density_ref, term_ref, projected, weighted, total):
+def tile_kernel(
+    starts, window_ref, values_ref, grads_ref, weights_ref, density_ref, term_ref, projected, weighted, total
+):
     step = pl.program_id(1)
     functions = values_ref.shape[2]
     projected[...] = jnp.dot(values_ref[0], window_ref[0], preferred_element_type=jnp.float32)
@@ -137,10 +79,19 @@
 
     @pl.when(step == pl.num_programs(1) - 1)
     def _():
-        term_ref[0] = total[...] + total[...].T
-
-
-def tile_terms(values, grads, quadrature, window_blocks):
+        total[...] = total[...] + total[...].T
+        shift = 4 * (starts[pl.program_id(0)] % 2)
+        for holder in range(COLS):
+            for which in range(2):
+                piece = holder + 8 * which - shift
+                inside = (piece >= 0) & (piece < 12)
+                first_row = pl.multiple_of(SLICE * jnp.where(inside, piece, 0), SLICE)
+                term_ref[holder, 0, which] = jnp.where(
+                    inside, total[pl.ds(first_row, SLICE), :], 0.0
+                ).astype(jnp.bfloat16)
+
+
+def tile_terms(windows, values, grads, quadrature, window_blocks):
     tiles, points, functions = values.shape
     steps = points // POINT_BLOCK
     packed_weights = jnp.swapaxes(quadrature.reshape(tiles, steps, 128, 8), 2, 3)
@@ -149,6 +100,7 @@
         name="tile_terms",
         grid=(tiles, steps),
         in_specs=[
+            pl.BlockSpec(memory_space=pltpu.SMEM),
             pl.BlockSpec((1, functions, functions), lambda t, s: (t, 0, 0)),
             pl.BlockSpec((1, POINT_BLOCK, functions), lambda t, s: (t, s, 0)),
             pl.BlockSpec((3, 1, POINT_BLOCK, functions), lambda t, s: (0, t, s, 0)),
@@ -156,11 +108,11 @@
         ],
         out_specs=[
             pl.BlockSpec((1, 1, 8, 128), lambda t, s: (t, s, 0, 0)),
-            pl.BlockSpec((1, functions, functions), lambda t, s: (t, 0, 0)),
+            pl.BlockSpec((COLS, 1, 2, SLICE, functions), lambda t, s: (0, t, 0, 0, 0)),
         ],
         out_shape=[
             jax.ShapeDtypeStruct((tiles, steps, 8, 128), jnp.float32),
-            jax.ShapeDtypeStruct((tiles, functions, functions), jnp.float32),
+            jax.ShapeDtypeStruct((COLS, tiles, 2, SLICE, functions), jnp.bfloat16),
         ],
         scratch_shapes=[
             pltpu.VMEM((POINT_BLOCK, functions), jnp.float32),
@@ -175,7 +127,7 @@
             bytes_accessed=8 * tiles * points * functions,
             transcendentals=0,
         ),
-    )(window_blocks, values, grads, packed_weights)
+    )(windows, window_blocks, values, grads, packed_weights)
     return jnp.swapaxes(density, 2, 3).reshape(tiles, points), terms
 
 
@@ -231,7 +183,10 @@
 def purify_kernel(
     density,
     kept,
+    starts,
     purified,
+    window_blocks,
+    all_starts,
     first,
     second,
     squares,
@@ -250,6 +205,16 @@
     recv_out,
     kept_sems,
     own_sem,
+    near,
+    ready,
+    staged,
+    start_words,
+    send_starts,
+    recv_starts,
+    send_edge,
+    recv_edge,
+    send_window,
+    recv_window,
 ):
     q = lax.axis_index("row")
     c = lax.axis_index("col")
@@ -288,9 +253,37 @@
         def _():
             greet(q + 2, other)
 
+        @pl.when((m > 0) & (h == 0) & (((c == 0) & (other <= 3)) | ((c >= 4) & (other == 7))))
+        def _():
+            greet(q - 1, other)
+
+        @pl.when((m < 7) & (h == 1) & (((c == 7) & (other >= 4)) | ((c <= 3) & (other == 0))))
+        def _():
+            greet(q + 1, other)
+
     lower = jnp.where(m > 0, jnp.where(h == 0, 2, jnp.where(c <= 1, 8, 0)), 0)
     upper = jnp.where(m < 7, jnp.where(h == 1, 2, jnp.where(c >= 6, 8, 0)), 0)
-    pl.semaphore_wait(barrier, 15 + lower + upper)
+    lower_side = jnp.where((m > 0) & (h == 0), jnp.where(c == 0, 4, jnp.where(c >= 4, 1, 0)), 0)
+    upper_side = jnp.where((m < 7) & (h == 1), jnp.where(c == 7, 4, jnp.where(c <= 3, 1, 0)), 0)
+    pl.semaphore_wait(barrier, 15 + lower + upper + lower_side + upper_side)
+
+    def start_copy(other):
+        return pltpu.make_async_remote_copy(
+            starts,
+            all_starts.at[c],
+            send_starts.at[other],
+            recv_starts,
+            device_id={"row": q, "col": other},
+            device_id_type=pl.DeviceIdType.MESH,
+        )
+
+    @pl.loop(0, COLS)
+    def _(other):
+        @pl.when(other != c)
+        def _():
+            start_copy(other).start()
+
+    pltpu.make_async_copy(starts, all_starts.at[c], recv_starts).start()
 
     kept_copy = pltpu.make_async_remote_copy(
         kept, kept_other, kept_sems.at[0], kept_sems.at[1], **sibling
@@ -453,7 +446,101 @@
             def _():
                 act(pltpu.make_async_copy(source, landing, recv_out.at[c % 4]), False)
 
+    def edge_copies(act):
+        for side, reach, slot in ((0, -1, 5), (3, 1, 0)):
+            row = 2 * m + c // 4 + reach
+
+            @pl.when((c % 4 == side) & (row >= 0) & (row < 16))
+            def _():
+                for u in range(4):
+                    here = (row == q) & (4 * h + u == c)
+                    source = final.at[pl.ds(1, 3), pl.ds(SLICE * u, SLICE)]
+                    landing = near.at[slot]
+                    arrived = recv_edge.at[slot // 5]
+
+                    @pl.when(jnp.logical_not(here))
+                    def _():
+                        act(
+                            pltpu.make_async_remote_copy(
+                                source,
+                                landing,
+                                send_edge.at[u],
+                                arrived,
+                                device_id={"row": row, "col": 4 * h + u},
+                                device_id_type=pl.DeviceIdType.MESH,
+                            ),
+                            True,
+                        )
+
+                    @pl.when(here)
+                    def _():
+                        act(pltpu.make_async_copy(source, landing, arrived), False)
+
+    edge_copies(lambda copy, remote: copy.start())
     out_copies(lambda copy, remote: copy.start())
+    pltpu.make_async_copy(all_starts, all_starts, recv_starts).wait()
+    words = pltpu.make_async_copy(all_starts, start_words, own_sem)
+    words.start()
+    words.wait()
+    for local in range(4):
+        part = purified.at[local]
+        pltpu.make_async_copy(part, part, recv_out.at[local]).wait()
+        near[local + 1] = purified[local, pl.ds(1, 3)]
+
+    for side in range(2):
+        part = near.at[5 * side]
+        reached = (q < 15) if side else (q > 0)
+
+        @pl.when(reached)
+        def _():
+            pltpu.make_async_copy(part, part, recv_edge.at[side]).wait()
+
+        @pl.when(jnp.logical_not(reached))
+        def _():
+            near[5 * side] = jnp.zeros((3, SLICE, WIDTH), jnp.bfloat16)
+
+    def window_copy(other):
+        return pltpu.make_async_remote_copy(
+            ready.at[other],
+            staged.at[c],
+            send_window.at[other],
+            recv_window,
+            device_id={"row": q, "col": other},
+            device_id_type=pl.DeviceIdType.MESH,
+        )
+
+    @pl.loop(0, COLS)
+    def _(other):
+        for t in range(2):
+            start = start_words[other, 0, t]
+            lead = jnp.clip(start // 2 - (4 * q - 1), 0, 4)
+            odd = (start % 2) == 1
+            for which in range(2):
+                left = near[lead + which, 1 - which]
+                right = near[lead + which, 2 - which]
+                for third, even_part, odd_part in (
+                    (0, left[:, :128], left[:, 128:]),
+                    (1, left[:, 128:], right[:, :128]),
+                    (2, right[:, :128], right[:, 128:]),
+                ):
+                    ready[other, t, which, :, 128 * third : 128 * third + 128] = jnp.where(
+                        odd, odd_part, even_part
+                    )
+
+        @pl.when(other != c)
+        def _():
+            window_copy(other).start()
+
+        @pl.when(other == c)
+        def _():
+            pltpu.make_async_copy(ready.at[other], staged.at[c], recv_window).start()
+
+    pltpu.make_async_copy(staged, staged, recv_window).wait()
+    for t in range(2):
+        shift = 4 * (start_words[c, 0, t] % 2)
+        for u in range(12):
+            at = shift + u
+            window_blocks[t, SLICE * u : SLICE * u + SLICE, :] = staged[at % 8, t, at // 8]
 
     @pl.loop(0, 4)
     def _(local):
@@ -481,24 +568,31 @@
             second_pass(role).wait_send()
 
     out_copies(lambda copy, remote: copy.wait_send() if remote else None)
-    for local in range(4):
-        part = purified.at[local]
-        pltpu.make_async_copy(part, part, recv_out.at[local]).wait()
-
-
-def purify(density, pattern):
-    blocks, diagonals, width, across = density.shape
-    kept = jnp.broadcast_to(
-        jnp.pad((pattern > 0).astype(jnp.float32), ((0, 0), (0, 3)))[:, :, None], (blocks, 8, WIDTH)
-    )
+    edge_copies(lambda copy, remote: copy.wait_send() if remote else None)
+
+    @pl.loop(0, COLS)
+    def _(other):
+        @pl.when(other != c)
+        def _():
+            start_copy(other).wait_send()
+            window_copy(other).wait_send()
+
+
+def purify(density, kept, windows):
+    starts = jnp.broadcast_to(jnp.pad(windows, (0, 126))[None], (8, 128))
+    functions = 3 * HALF
     bf16, dma = jnp.bfloat16, pltpu.SemaphoreType.DMA
     vmem = pl.BlockSpec(memory_space=pltpu.VMEM)
     return pl.pallas_call(
         purify_kernel,
         name="purify",
-        in_specs=[vmem, vmem],
-        out_specs=vmem,
-        out_shape=jax.ShapeDtypeStruct(density.shape, bf16),
+        in_specs=[vmem, vmem, vmem],
+        out_specs=[vmem, vmem, vmem],
+        out_shape=[
+            jax.ShapeDtypeStruct(density.shape, bf16),
+            jax.ShapeDtypeStruct((2, functions, functions), bf16),
+            jax.ShapeDtypeStruct((COLS, 8, 128), jnp.int32),
+        ],
         scratch_shapes=[
             pltpu.VMEM((12, WIDTH, WIDTH), bf16),
             pltpu.VMEM((19, WIDTH, WIDTH), bf16),
@@ -518,73 +612,189 @@
             dma((4,)),
             dma((2,)),
             dma(()),
+            pltpu.VMEM((6, 3, SLICE, WIDTH), bf16),
+            pltpu.VMEM((COLS, 2, 2, SLICE, functions), bf16),
+            pltpu.VMEM((COLS, 2, 2, SLICE, functions), bf16),
+            pltpu.SMEM((COLS, 8, 128), jnp.int32),
+            dma((COLS,)),
+            dma(()),
+            dma((4,)),
+            dma((2,)),
+            dma((COLS,)),
+            dma(()),
         ],
         compiler_params=pltpu.CompilerParams(
             collective_id=0, has_side_effects=True, vmem_limit_bytes=40 * 1024 * 1024
         ),
-    )(density, kept)
-
-
-def window_of(band_three, lead, offset, functions):
-    paired = lax.dynamic_slice_in_dim(band_three, lead, 2, 0)
-    upper = jnp.concatenate([paired[0, 1], paired[0, 2]], axis=1)
-    lower = jnp.concatenate([paired[1, 0], paired[1, 1]], axis=1)
-    dense = jnp.concatenate([upper, lower], axis=0)
-    return lax.dynamic_slice(dense, (offset, offset), (functions, functions))
-
-
-def spread_term(summed, term, lead, offset):
-    width = summed.shape[2]
-    dense = lax.dynamic_update_slice(
-        jnp.zeros((2 * width, 2 * width), summed.dtype), term, (offset, offset)
+    )(density, kept, starts)
+
+
+def gather_terms_kernel(terms, kept, starts, matrix, staged, sums, edges, arrived, send, recv, send_edge, recv_edge):
+    q = lax.axis_index("row")
+    c = lax.axis_index("col")
+    barrier = pltpu.get_barrier_semaphore()
+
+    def greet(row, col):
+        pl.semaphore_signal(
+            barrier, inc=1, device_id={"row": row, "col": col}, device_id_type=pl.DeviceIdType.MESH
+        )
+
+    @pl.loop(0, COLS)
+    def _(other):
+        @pl.when(other != c)
+        def _():
+            greet(q, other)
+
+    @pl.when(q > 0)
+    def _():
+        greet(q - 1, c)
+
+    @pl.when(q < 15)
+    def _():
+        greet(q + 1, c)
+
+    for s in range(COLS):
+        for t in range(2):
+            staged[s, t, 2] = jnp.zeros((SLICE, 3 * HALF), jnp.bfloat16)
+
+    pl.semaphore_wait(barrier, 7 + jnp.where(q > 0, 1, 0) + jnp.where(q < 15, 1, 0))
+
+    def term_copy(other):
+        return pltpu.make_async_remote_copy(
+            terms.at[other],
+            staged.at[c, :, pl.ds(0, 2)],
+            send.at[other],
+            recv,
+            device_id={"row": q, "col": other},
+            device_id_type=pl.DeviceIdType.MESH,
+        )
+
+    @pl.loop(0, COLS)
+    def _(other):
+        @pl.when(other != c)
+        def _():
+            term_copy(other).start()
+
+    pltpu.make_async_copy(terms.at[c], staged.at[c, :, pl.ds(0, 2)], recv).start()
+    whole = staged.at[:, :, pl.ds(0, 2)]
+    pltpu.make_async_copy(whole, whole, recv).wait()
+
+    @pl.loop(0, 5)
+    def _(lead):
+        for which in range(2):
+            for odd in range(2):
+                total = None
+                for s in range(COLS):
+                    for t in range(2):
+                        start = starts[2 * s + t]
+                        chosen = (start // 2 - (4 * q - 1) == lead) & (start % 2 == odd)
+                        piece = staged[s, t, jnp.where(chosen, which, 2)].astype(jnp.float32)
+                        total = piece if total is None else total + piece
+                sums[lead, which, odd] = total
+
+    def block_row(r):
+        wide = [jnp.zeros((SLICE, HALF), jnp.float32) for _ in range(6)]
+        for which in range(2):
+            if 0 <= r - which < 5:
+                for odd in range(2):
+                    piece = sums[r - which, which, odd]
+                    for third in range(3):
+                        place = 2 + odd - 2 * which + third
+                        wide[place] = wide[place] + piece[:, HALF * third : HALF * third + HALF]
+        return [jnp.concatenate(wide[2 * d : 2 * d + 2], axis=1) for d in range(3)]
+
+    for side in range(2):
+        for d, block in enumerate(block_row(5 * side)):
+            edges[side, d] = block.astype(jnp.bfloat16)
+
+    def edge_copy(side):
+        return pltpu.make_async_remote_copy(
+            edges.at[side],
+            arrived.at[1 - side],
+            send_edge.at[side],
+            recv_edge.at[1 - side],
+            device_id={"row": q + 2 * side - 1, "col": c},
+            device_id_type=pl.DeviceIdType.MESH,
+        )
+
+    for side in range(2):
+        reached = (q < 15) if side else (q > 0)
+
+        @pl.when(reached)
+        def _():
+            edge_copy(side).start()
+
+        @pl.when(jnp.logical_not(reached))
+        def _():
+            arrived[side] = jnp.zeros((3, SLICE, WIDTH), jnp.bfloat16)
+
+    for local in (1, 2, 0, 3):
+        if local in (0, 3):
+            side = local // 3
+            reached = (q < 15) if side else (q > 0)
+
+            @pl.when(reached)
+            def _():
+                edge_copy(1 - side).wait_recv()
+
+        blocks = block_row(local + 1)
+        matrix[local, 0] = jnp.zeros((SLICE, WIDTH), jnp.float32)
+        matrix[local, 4] = jnp.zeros((SLICE, WIDTH), jnp.float32)
+        for d in range(3):
+            block = blocks[d]
+            if local in (0, 3):
+                block = block + arrived[local // 3, d].astype(jnp.float32)
+            matrix[local, d + 1] = jnp.where(kept[local, d + 1 : d + 2] > 0, block, 0.0)
+
+    for side in range(2):
+        reached = (q < 15) if side else (q > 0)
+
+        @pl.when(reached)
+        def _():
+            edge_copy(side).wait_send()
+
+    @pl.loop(0, COLS)
+    def _(other):
+        @pl.when(other != c)
+        def _():
+            term_copy(other).wait_send()
+
+
+def gather_terms(terms, kept, starts):
+    bf16, dma = jnp.bfloat16, pltpu.SemaphoreType.DMA
+    vmem = pl.BlockSpec(memory_space=pltpu.VMEM)
+    functions = 3 * HALF
+    return pl.pallas_call(
+        gather_terms_kernel,
+        name="gather_terms",
+        in_specs=[vmem, vmem, pl.BlockSpec(memory_space=pltpu.SMEM)],
+        out_specs=vmem,
+        out_shape=jax.ShapeDtypeStruct((4, BAND, SLICE, WIDTH), jnp.float32),
+        scratch_shapes=[
+            pltpu.VMEM((COLS, 2, 3, SLICE, functions), bf16),
+            pltpu.VMEM((5, 2, 2, SLICE, functions), jnp.float32),
+            pltpu.VMEM((2, 3, SLICE, WIDTH), bf16),
+            pltpu.VMEM((2, 3, SLICE, WIDTH), bf16),
+            dma((COLS,)),
+            dma(()),
+            dma((2,)),
+            dma((2,)),
+        ],
+        compiler_params=pltpu.CompilerParams(
+            collective_id=1, has_side_effects=True, vmem_limit_bytes=40 * 1024 * 1024
+        ),
+    )(terms, kept, starts)
+
+
+def on_device(density, pattern, windows, basis_values, basis_grads, weights):
+    band = (pattern > 0)[:, :, None, None]
+    current = jnp.where(band, density, jnp.zeros_like(density))
+    kept = jnp.broadcast_to(
+        jnp.pad((pattern > 0).astype(jnp.float32), ((0, 0), (0, 3)))[:, :, None], (4, 8, WIDTH)
     )
-    nothing = jnp.zeros((width, width), summed.dtype)
-    upper = jnp.stack([nothing, dense[:width, :width], dense[:width, width:]])
-    lower = jnp.stack([dense[width:, :width], dense[width:, width:], nothing])
-    increment = jnp.stack([upper, lower])
-    paired = lax.dynamic_slice_in_dim(summed, lead, 2, 0)
-    return lax.dynamic_update_slice_in_dim(summed, paired + increment, lead, 0)
-
-
-def edge_rows(summed):
-    blocks = summed.shape[0] - 2
-    from_above = shifted_2(summed[0].astype(jnp.bfloat16), "row", -1).astype(jnp.float32)
-    from_below = shifted_2(summed[blocks + 1].astype(jnp.bfloat16), "row", 1).astype(jnp.float32)
-    own_rows = summed[1 : blocks + 1]
-    return jnp.concatenate(
-        [
-            own_rows[:1] + from_below[None],
-            own_rows[1 : blocks - 1],
-            own_rows[blocks - 1 :] + from_above[None],
-        ],
-        axis=0,
-    )
-
-
-def on_device(density, pattern, windows, basis_values, basis_grads, weights):
-    row_index = lax.axis_index("row")
-    band_rows = density.shape[0]
-    functions = basis_values.shape[2]
-    step_size = functions // 3
-    kept = (pattern > 0)[:, :, None, None]
-    current = jnp.where(kept, density, jnp.zeros_like(density))
-    current = purify(current, pattern)
-    rows_band = gather_directly(current[:, 1:4], COL, 2)
-    near = padded(rows_band, (("row", 0),), 1)
-    tiles_here = windows.shape[0]
-    block_size = near.shape[2]
-    leads = [windows[t] // 2 - (band_rows * row_index - 1) for t in range(tiles_here)]
-    offsets = [windows[t] % 2 * step_size for t in range(tiles_here)]
-    window_blocks = jnp.stack(
-        [window_of(near, leads[t], offsets[t], functions) for t in range(tiles_here)]
-    )
-    densities, contributions = tile_terms(basis_values, basis_grads, weights, window_blocks)
-    local_terms = jnp.zeros((band_rows + 2, 3, block_size, block_size), jnp.float32)
-    for t in range(tiles_here):
-        local_terms = spread_term(local_terms, contributions[t], leads[t], offsets[t])
-    owner_part = scatter_axes(local_terms.astype(jnp.bfloat16), (COL,), (0,), 2).astype(jnp.float32)
-    mine = edge_rows(owner_part)
-    xc_matrix = jnp.where(kept, jnp.pad(mine, ((0, 0), (1, 1), (0, 0), (0, 0))), 0.0)
+    current, window_blocks, all_starts = purify(current, kept, windows)
+    densities, terms = tile_terms(windows, basis_values, basis_grads, weights, window_blocks)
+    xc_matrix = gather_terms(terms, kept, all_starts[:, 0, :2].reshape(-1))
     return (current, xc_matrix, densities)
 
 

time: 227 us -> 120 us (0.53)
  waiting for transfers between devices: 74.8 us -> 0 us
  Pallas kernels: 70.7 us -> 109 us
  blocking collectives: 27 us -> 0 us
  between operations: 19.6 us -> 0.69 us
  starting transfers between devices: 14.3 us -> 0 us
  other arithmetic: 9.54 us -> 1.76 us
    reduce_scatter x1 -> x0, waiting for transfers between devices: 72.3 us -> none  [sum_in_order(): pieces = lax.psum_scatter(pieces, axes[k], scatter_dimension=0, tiled=True)]
    pallas_call x1 -> x2, Pallas kernels: 48 us -> 85.1 us  [the longest x1 60.2 us: purify(): pl.pallas_call(purify_kernel, name='purify', in_specs=[vmem, vmem, vmem],...]
    all_to_all x1 -> x0, blocking collectives: 27 us -> none  [sent_to_all(): lax.all_to_all(jnp.broadcast_to(value[None], (length, *value.shape)), axi...]
    ppermute x4 -> x0, starting transfers between devices: 14.3 us -> none  [the longest x2 7.11 us: shifted_2(): return lax.ppermute(value, axis, pairs)]
    unnamed x9 -> x6, local copies, waits for them, and re-layouts: 0.74 us -> 5 us
    another operation x3 -> x0, other arithmetic: 3.09 us -> none  [the longest x2 2.76 us: on_device(): jnp.stack([window_of(near, leads[t], offsets[t], functions) for t in rang...]
    slice x4 -> x1, local copies, waits for them, and re-layouts: 2.83 us -> 0.02 us  [on_device(): xc_matrix = gather_terms(terms, kept, all_starts[:, 0, :2].reshape(-1))]
    ppermute x4 -> x0, waiting for transfers between devices: 2.44 us -> none  [the longest x2 2.43 us: shifted_2(): return lax.ppermute(value, axis, pairs)]
  transfers between devices with their start and end apart: 5 -> 0, of which waited for: 2 -> 0; matrix products, arithmetic and copies ran while one was open for 1% -> 0% of each run, Pallas kernels for 0% -> 0%
where the time goes in v3:
time: 120 us; the launch traced here: 119 us
  Pallas kernels  109 us (91%)
  local copies, waits for them, and re-layouts  8.15 us (7%)
  other arithmetic  1.76 us (1%)
    pallas_call x1, Pallas kernels, purify(): pl.pallas_call(purify_kernel, name='purify', in_specs=[vmem, vmem, vmem],...  60.2 us
    pallas_call x1, Pallas kernels, gather_terms(): pl.pallas_call(gather_terms_kernel, name='gather_terms', in_specs=[vmem,...  24.9 us
    pallas_call x1, Pallas kernels, tile_terms(): pl.pallas_call(tile_kernel, name='tile_terms', grid=(tiles, steps), in_sp...  23.8 us
    unnamed x6, local copies, waits for them, and re-layouts  5 us

profile of v3, /device:TPU:1, one launch (start us, length us, event | category | flops | bytes accessed | tf_op | source)
XLA Modules:
  0.0 119.5 jit_solution(3007043714767932443)
XLA Ops:
  0.6 0.7 broadcast_compare_fusion
  1.3 0.7 pad.13
  2.0 0.1 broadcast_in_dim.26.kept
  2.1 1.1 broadcast_select_fusion.density
  3.1 1.1 reshape.15
  4.2 0.2 copy.9
  4.4 60.2 %purify.1 = (bf16[4,5,32,256]{3,2,1,0:T(8,128)(2,1)S(1)}, bf16[2,384,384]{2,1,0:T(8,128)(2,1)S(1)}, s32[8,8,128]{2,1,0:T(8,128)S(1)}) custom-call(bf16[4,5,32,256]{3,2,1,0:T(8,128)(2,1)S(1)} %broadcast_select_fusion.density, f32[4,8,256]{2,1,0:T(8,128)S(1)} %broadcast_in_dim.26.kept, s32[8,128]{1,0:T(8,128)S(1)} %broadcast_in_dim.27.starts), custom_call_target="tpu_custom_call" | custom-call | tf_op jit(solution)/shard_map/purify/pallas_call | solution.py:586
  64.5 0.1 reshape_squeeze.3.starts
  64.6 0.0 copy-start
  64.6 2.8 %copy-done = bf16[2,4096,384]{2,1,0:T(8,128)(2,1)S(1)} copy-done((bf16[2,4096,384]{2,1,0:T(8,128)(2,1)S(1)}, bf16[2,4096,384]{2,1,0:T(8,128)(2,1)}, u32[]{:S(2)}) %copy-start) | copy-done | bytes 6291480
  67.4 0.0 copy-start.1
  67.4 0.7 copy-done.1
  68.1 23.8 %tile_terms.1 = (f32[2,4,8,128]{3,2,1,0:T(8,128)S(1)}, bf16[8,2,2,32,384]{4,3,2,1,0:T(8,128)(2,1)S(1)}) custom-call(s32[2]{0:T(128)S(1)} %copy-done.1, bf16[2,384,384]{2,1,0:T(8,128)(2,1)S(1)} %get-tuple-element.9.window_ref, bf16[2,4096,384]{2,1,0:T(8,128)(2,1)S(1)} %copy-done, bf16[3,2,4096,384]{3,2,1,0:T(8,128)(2,1)} %grads_ref.1, ...), custom_call_target="tpu_custom_call" | custom-call | flops 4831838208 | bytes 25165824 | tf_op jit(solution)/shard_map/tile_terms/pallas_call | solution.py:98
  91.9 24.9 %gather_terms.1 = f32[4,5,32,256]{3,2,1,0:T(8,128)S(1)} custom-call(bf16[8,2,2,32,384]{4,3,2,1,0:T(8,128)(2,1)S(1)} %get-tuple-element.10.terms, f32[4,8,256]{2,1,0:T(8,128)S(1)} %broadcast_in_dim.26.kept, s32[16]{0:T(128)S(1)} %reshape_squeeze.3.starts), custom_call_target="tpu_custom_call" | custom-call | tf_op jit(solution)/shard_map/gather_terms/pallas_call | solution.py:767
  116.8 0.2 copy.10
  117.0 0.9 reshape.16
  117.9 0.7 copy.13
  118.6 0.8 copy.14
  (3 shorter events, 0.0 us)
Async XLA Ops:
  64.6 2.8 %copy-start = (bf16[2,4096,384]{2,1,0:T(8,128)(2,1)S(1)}, bf16[2,4096,384]{2,1,0:T(8,128)(2,1)}, u32[]{:S(2)}) copy-start(bf16[2,4096,384]{2,1,0:T(8,128)(2,1)} %values_ref.1) | copy-start | bytes 18874372
  67.4 0.7 copy-start.1

commit v4 on v3

v4 whole, which is shorter than its diff:
```python
import jax
import jax.numpy as jnp
from jax import lax
from jax.experimental import pallas as pl
from jax.experimental.pallas import tpu as pltpu
from jax.sharding import PartitionSpec as P

COL = "col"
ROW_COL = ("row", "col")


slater_cx = 0.7386
kappa_pbe = 0.804
mu_pbe = 0.2195


POINT_BLOCK = 1024
STEPS = 4
LANES = 256
FUNCTIONS = 384


def potentials(density, grad_square):
    inverse_root = jnp.exp(jnp.log(density * density + 1.0) * (-1.0 / 3.0))
    inverse_two = inverse_root * inverse_root
    reduced = grad_square * (inverse_two * inverse_two)
    share = 1.0 / (1.0 + (mu_pbe / kappa_pbe) * reduced)
    enhance = 1.0 + kappa_pbe - kappa_pbe * share
    slope = mu_pbe * share * share
    by_density = (-slater_cx * 4.0 / 3.0) * inverse_root * density * (enhance - 2.0 * reduced * slope)
    by_gradient = -slater_cx * slope * inverse_two
    return by_density, by_gradient


BLOCKS = 64
BAND = 5
HALF = 128
WIDTH = 256
SLICE = 32
COLS = 8
FIRST_PIECES = {
    -2: ((2, 2, 0),),
    -1: ((2, 1, 2), (4, 1, 3)),
    0: ((0, 5, 4),),
    1: ((2, 2, 9),),
    2: ((2, 1, 11),),
}
FIRST_ROLE = {-2: (0, 2), -1: (2, 2), 0: (4, 5), 1: (9, 2), 2: (11, 1)}
FIRST_SLOT = {(-2, -2): 0, (-2, -1): 1, (-1, -1): 2, (-1, 1): 3, (1, 1): 9, (1, 2): 10, (2, 2): 11}
SECOND_ROLE = {-2: (0, 3, 2), -1: (3, 4, 1), 0: (7, 5, 0), 1: (12, 4, 0), 2: (16, 3, 0)}


def first_block(a, b):
    if a == 0:
        return 6 + b, False
    if b == 0:
        return 6 + a, True
    if (a, b) in FIRST_SLOT:
        return FIRST_SLOT[a, b], False
    return FIRST_SLOT[b, a], True


def second_block(a, b):
    return SECOND_ROLE[a][0] + b - max(-2, a - 2), False


def product(left, right, where):
    columns = []
    for b in range(-2, 3):
        total = None
        for a in range(max(-2, b - 2), min(2, b + 2) + 1):
            slot, flipped = where(a, b)
            term = lax.dot_general(
                left(a + 2),
                right[slot],
                (((1,), (1 if flipped else 0,)), ((), ())),
                preferred_element_type=jnp.float32,
            )
            total = term if total is None else total + term
        columns.append(total)
    return columns


def fused_kernel(
    density,
    pattern,
    windows,
    values,
    grads,
    weights,
    purified,
    matrix,
    densities,
    masked,
    kept,
    kept_other,
    starts,
    all_starts,
    start_words,
    natural,
    turned,
    first,
    second,
    squares,
    mine,
    final,
    near,
    ready,
    staged_first,
    staged_second,
    window,
    projected,
    weighted,
    total,
    rows_of,
    terms,
    gathered_first,
    gathered_second,
    sums,
    edges,
    arrived,
    load_sems,
    kept_sems,
    send_starts,
    recv_starts,
    send_first,
    recv_first,
    send_pass,
    recv_pass,
    send_second,
    recv_second,
    send_pass_second,
    recv_pass_second,
    own_sem,
    send_out,
    recv_out,
    send_edge,
    recv_edge,
    send_window,
    recv_window,
    send_terms,
    recv_terms,
    send_sum,
    recv_sum,
):
    staged, gathered = (staged_first, staged_second), (gathered_first, gathered_second)
    q = lax.axis_index("row")
    c = lax.axis_index("col")
    m = q // 2
    h = q % 2
    j = 2 * (c % 4) + c // 4
    i = 8 * m + j
    rows = pl.ds(pl.multiple_of(HALF * h, HALF), HALF)
    sibling = dict(device_id={"row": 2 * m + 1 - h, "col": c}, device_id_type=pl.DeviceIdType.MESH)

    def chip(block_row):
        return dict(
            device_id={"row": 2 * (block_row // 8) + h, "col": block_row % 2 * 4 + block_row % 8 // 2},
            device_id_type=pl.DeviceIdType.MESH,
        )

    def load(n):
        slot = n % 2
        tile, part = n // STEPS, pl.ds(pl.multiple_of(n % STEPS * POINT_BLOCK, POINT_BLOCK), POINT_BLOCK)
        return (
            pltpu.make_async_copy(values.at[tile, part], natural.at[slot, 0], load_sems.at[slot, 0]),
            pltpu.make_async_copy(grads.at[:, tile, part], natural.at[slot, pl.ds(1, 3)], load_sems.at[slot, 1]),
        )

    for n in range(2):
        for copy in load(n):
            copy.start()

    barrier = pltpu.get_barrier_semaphore()

    def greet(row, col):
        pl.semaphore_signal(
            barrier, inc=1, device_id={"row": row, "col": col}, device_id_type=pl.DeviceIdType.MESH
        )

    @pl.loop(0, COLS)
    def _(other):
        greet(2 * m + 1 - h, other)

        @pl.when(other != c)
        def _():
            greet(q, other)

        @pl.when((m > 0) & (((h == 0) & (other % 4 == 3)) | ((h == 1) & (c % 4 == 0))))
        def _():
            greet(q - 2, other)

        @pl.when((m < 7) & (((h == 1) & (other % 4 == 0)) | ((h == 0) & (c % 4 == 3))))
        def _():
            greet(q + 2, other)

        @pl.when((m > 0) & (h == 0) & (((c == 0) & (other <= 3)) | ((c >= 4) & (other == 7)) | (other == c)))
        def _():
            greet(q - 1, other)

        @pl.when((m < 7) & (h == 1) & (((c == 7) & (other >= 4)) | ((c <= 3) & (other == 0)) | (other == c)))
        def _():
            greet(q + 1, other)

    lower = jnp.where(m > 0, jnp.where(h == 0, 2, jnp.where(c % 4 == 0, 8, 0)), 0)
    upper = jnp.where(m < 7, jnp.where(h == 1, 2, jnp.where(c % 4 == 3, 8, 0)), 0)
    some = jnp.where((c >= 4) & (c <= 6), 2, 1)
    lower_side = jnp.where((m > 0) & (h == 0), jnp.where(c == 0, 4, some), 0)
    some = jnp.where((c >= 1) & (c <= 3), 2, 1)
    upper_side = jnp.where((m < 7) & (h == 1), jnp.where(c == 7, 4, some), 0)

    for local in range(4):
        for d in range(BAND):
            flag = pattern[local, d] > 0
            masked[local, d] = jnp.where(flag, density[local, d], jnp.zeros((SLICE, WIDTH), jnp.bfloat16))
            kept[local, d : d + 1] = jnp.where(flag, jnp.ones((1, WIDTH), jnp.float32), 0.0)
    lane = lax.broadcasted_iota(jnp.int32, (8, 128), 1)
    starts[...] = jnp.where(lane == 0, windows[0], windows[1])
    pl.semaphore_wait(barrier, 15 + lower + upper + lower_side + upper_side)

    def start_copy(other):
        return pltpu.make_async_remote_copy(
            starts,
            all_starts.at[c],
            send_starts.at[other],
            recv_starts,
            device_id={"row": q, "col": other},
            device_id_type=pl.DeviceIdType.MESH,
        )

    @pl.loop(0, COLS)
    def _(other):
        @pl.when(other != c)
        def _():
            start_copy(other).start()

    pltpu.make_async_copy(starts, all_starts.at[c], recv_starts).start()

    kept_copy = pltpu.make_async_remote_copy(
        kept, kept_other, kept_sems.at[0], kept_sems.at[1], **sibling
    )
    kept_copy.start()

    def first_copies(local, act):
        k = 4 * q + local
        place = pl.ds(pl.multiple_of(SLICE * c, SLICE), SLICE)
        index = 0
        for role, pieces in FIRST_PIECES.items():
            target = k - role
            valid = (target >= 0) & (target < BLOCKS)
            for diagonal, count, slot in pieces:
                source = masked.at[local, pl.ds(diagonal, count)]
                landing = first.at[pl.ds(slot, count), place]

                @pl.when(valid & (target != i))
                def _():
                    act(
                        pltpu.make_async_remote_copy(
                            source,
                            landing,
                            send_first.at[local, index],
                            recv_first.at[role + 2],
                            **chip(target),
                        ),
                        True,
                    )

                @pl.when(target == i)
                def _():
                    act(pltpu.make_async_copy(source, landing, recv_first.at[role + 2]), False)

                index += 1

    @pl.loop(0, 4)
    def _(local):
        first_copies(local, lambda copy, remote: copy.start())

    @pl.loop(0, 2 * STEPS)
    def _(n):
        for copy in load(n):
            copy.wait()
        for k in range(4):
            turned[n, k] = natural[n % 2, k].T

        @pl.when(n < 2 * STEPS - 2)
        def _():
            for copy in load(n + 2):
                copy.start()

    def pass_on(role):
        slot, count = FIRST_ROLE[role]
        part = first.at[pl.ds(slot, count)]
        return pltpu.make_async_remote_copy(
            part, part, send_pass.at[role + 2], recv_pass.at[role + 2], **sibling
        )

    order = (0, -1, 1, -2, 2)
    for role in order:
        slot, count = FIRST_ROLE[role]
        part = first.at[pl.ds(slot, count)]
        k = i + role
        valid = (k >= 0) & (k < BLOCKS)

        @pl.when(valid & ((k // 4) % 2 == h))
        def _():
            pltpu.make_async_copy(part, part, recv_first.at[role + 2]).wait()
            pass_on(role).start()

        @pl.when(jnp.logical_not(valid))
        def _():
            first[pl.ds(slot, count)] = jnp.zeros((count, WIDTH, WIDTH), jnp.bfloat16)
            start, number, _ = SECOND_ROLE[role]
            second[pl.ds(start, number)] = jnp.zeros((number, WIDTH, WIDTH), jnp.bfloat16)

    for role in order:
        k = i + role

        @pl.when((k >= 0) & (k < BLOCKS) & ((k // 4) % 2 != h))
        def _():
            pass_on(role).wait_recv()

    kept_copy.wait()
    near_kept = kept[j % 4]
    far_kept = kept_other[j % 4]
    mask = jnp.where(h == j // 4, near_kept, far_kept)

    def iterate(left, right, where, result):
        for d, total in enumerate(product(left, right, where)):
            squares[d] = jnp.where(mask[d : d + 1] > 0, total, 0.0).astype(jnp.bfloat16)
        for d, total in enumerate(product(lambda a: squares[a], right, where)):
            value = 3.0 * squares[d].astype(jnp.float32) - 2.0 * total
            result[d] = jnp.where(mask[d : d + 1] > 0, value, 0.0).astype(jnp.bfloat16)

    iterate(lambda a: first[4 + a, rows, :], first, first_block, mine)

    own = pltpu.make_async_copy(mine, second.at[pl.ds(7, 5), rows], own_sem)
    own.start()
    own_far = pltpu.make_async_remote_copy(
        mine, second.at[pl.ds(7, 5), rows], send_pass_second.at[2], recv_pass_second.at[2], **sibling
    )
    own_far.start()

    def second_copy(role):
        start, number, diagonal = SECOND_ROLE[role]
        return pltpu.make_async_remote_copy(
            mine.at[pl.ds(diagonal, number)],
            second.at[pl.ds(start, number), rows],
            send_second.at[role + 2],
            recv_second.at[role + 2],
            **chip(i - role),
        )

    def second_pass(role):
        start, number, _ = SECOND_ROLE[role]
        part = second.at[pl.ds(start, number), rows]
        return pltpu.make_async_remote_copy(
            part, part, send_pass_second.at[role + 2], recv_pass_second.at[role + 2], **sibling
        )

    others = (-2, 2, -1, 1)
    for role in others:
        target = i - role

        @pl.when((target >= 0) & (target < BLOCKS))
        def _():
            second_copy(role).start()

    for role in (-1, 1, -2, 2):
        k = i + role

        @pl.when((k >= 0) & (k < BLOCKS))
        def _():
            second_copy(role).wait_recv()
            second_pass(role).start()

    for role in (-1, 1, -2, 2):
        k = i + role

        @pl.when((k >= 0) & (k < BLOCKS))
        def _():
            second_pass(role).wait_recv()

    own.wait()
    own_far.wait_recv()
    iterate(lambda a: mine[a], second, second_block, final)

    def out_copies(part, act):
        diagonal, count = ((1, 3), (0, 1), (4, 1))[part]
        for u in range(4):
            source = final.at[pl.ds(diagonal, count), pl.ds(SLICE * u, SLICE)]
            landing = purified.at[j % 4, pl.ds(diagonal, count)]
            row, col = 2 * m + j // 4, 4 * h + u
            here = (row == q) & (col == c)

            @pl.when(jnp.logical_not(here))
            def _():
                act(
                    pltpu.make_async_remote_copy(
                        source,
                        landing,
                        send_out.at[part, u],
                        recv_out.at[part, j % 4],
                        device_id={"row": row, "col": col},
                        device_id_type=pl.DeviceIdType.MESH,
                    ),
                    True,
                )

            @pl.when(here)
            def _():
                act(pltpu.make_async_copy(source, landing, recv_out.at[part, j % 4]), False)

    def edge_copies(act):
        for side, reach, slot in ((0, -1, 5), (3, 1, 0)):
            row = 2 * m + j // 4 + reach

            @pl.when((j % 4 == side) & (row >= 0) & (row < 16))
            def _():
                for u in range(4):
                    here = (row == q) & (4 * h + u == c)
                    source = final.at[pl.ds(1, 3), pl.ds(SLICE * u, SLICE)]
                    landing = near.at[slot]
                    arrived = recv_edge.at[slot // 5]

                    @pl.when(jnp.logical_not(here))
                    def _():
                        act(
                            pltpu.make_async_remote_copy(
                                source,
                                landing,
                                send_edge.at[u],
                                arrived,
                                device_id={"row": row, "col": 4 * h + u},
                                device_id_type=pl.DeviceIdType.MESH,
                            ),
                            True,
                        )

                    @pl.when(here)
                    def _():
                        act(pltpu.make_async_copy(source, landing, arrived), False)

    edge_copies(lambda copy, remote: copy.start())
    out_copies(0, lambda copy, remote: copy.start())
    pltpu.make_async_copy(all_starts, all_starts, recv_starts).wait()
    words = pltpu.make_async_copy(all_starts, start_words, own_sem)
    words.start()
    words.wait()
    for local in range(4):
        part = purified.at[local, pl.ds(1, 3)]
        pltpu.make_async_copy(part, part, recv_out.at[0, local]).wait()
        near[local + 1] = purified[local, pl.ds(1, 3)]

    for side in range(2):
        part = near.at[5 * side]
        reached = (q < 15) if side else (q > 0)

        @pl.when(reached)
        def _():
            pltpu.make_async_copy(part, part, recv_edge.at[side]).wait()

        @pl.when(jnp.logical_not(reached))
        def _():
            near[5 * side] = jnp.zeros((3, SLICE, WIDTH), jnp.bfloat16)

    def window_copy(other, t):
        return pltpu.make_async_remote_copy(
            ready.at[other, t],
            staged[t].at[c],
            send_window.at[other, t],
            recv_window.at[t],
            device_id={"row": q, "col": other},
            device_id_type=pl.DeviceIdType.MESH,
        )

    for t in range(2):

        @pl.loop(1, COLS + 1)
        def _(step):
            other = (c + step) % COLS
            start = start_words[other, 0, t]
            lead = jnp.clip(start // 2 - (4 * q - 1), 0, 4)
            odd = (start % 2) == 1
            for which in range(2):
                left = near[lead + which, 1 - which]
                right = near[lead + which, 2 - which]
                for third, even_part, odd_part in (
                    (0, left[:, :128], left[:, 128:]),
                    (1, left[:, 128:], right[:, :128]),
                    (2, right[:, :128], right[:, 128:]),
                ):
                    ready[other, t, which, :, 128 * third : 128 * third + 128] = jnp.where(
                        odd, odd_part, even_part
                    )

            @pl.when(other != c)
            def _():
                window_copy(other, t).start()

            @pl.when(other == c)
            def _():
                pltpu.make_async_copy(ready.at[other, t], staged[t].at[c], recv_window.at[t]).start()

    for part in (1, 2):
        out_copies(part, lambda copy, remote: copy.start())

    def term_copy(other, t):
        return pltpu.make_async_remote_copy(
            terms.at[other, t],
            gathered[t].at[c, pl.ds(0, 2)],
            send_terms.at[other, t],
            recv_terms.at[t],
            device_id={"row": q, "col": other},
            device_id_type=pl.DeviceIdType.MESH,
        )

    for s in range(COLS):
        for t in range(2):
            gathered[t][s, 2] = jnp.zeros((SLICE, FUNCTIONS), jnp.bfloat16)

    rows_of[12] = jnp.zeros((SLICE, FUNCTIONS), jnp.bfloat16)

    for t in range(2):
        part = staged[t]
        pltpu.make_async_copy(part, part, recv_window.at[t]).wait()
        shift = 4 * (start_words[c, 0, t] % 2)
        for u in range(12):
            at = shift + u
            window[SLICE * u : SLICE * u + SLICE, :] = staged[t][at % 8, at // 8]
        window[...] = window[...].T
        total[...] = jnp.zeros_like(total)
        weighted[1] = jnp.zeros((FUNCTIONS, POINT_BLOCK), jnp.bfloat16)
        projected[0] = jnp.dot(window[...], turned[STEPS * t, 0], preferred_element_type=jnp.float32)

        @pl.loop(0, STEPS)
        def _(s):
            n = STEPS * t + s
            now, later = s % 2, (s + 1) % 2
            ahead = STEPS * t + jnp.minimum(s + 1, STEPS - 1)
            behind = STEPS * t + jnp.maximum(s - 1, 0)
            projected[later] = jnp.dot(window[...], turned[ahead, 0], preferred_element_type=jnp.float32)
            total[...] += lax.dot_general(
                turned[behind, 0], weighted[later], (((1,), (1,)), ((), ())), preferred_element_type=jnp.float32
            )
            for piece in range(POINT_BLOCK // LANES):
                lanes = slice(piece * LANES, piece * LANES + LANES)
                points = pl.ds(pl.multiple_of(s * POINT_BLOCK + piece * LANES, LANES), LANES)
                x = projected[now, :, lanes]
                reduced = [
                    jnp.sum(x * turned[n, k, :, lanes].astype(jnp.float32), axis=0, keepdims=True)
                    for k in range(4)
                ]
                point_density = reduced[0] / FUNCTIONS
                slopes = [2.0 * r / FUNCTIONS for r in reduced[1:]]
                grad_square = slopes[0] * slopes[0] + slopes[1] * slopes[1] + slopes[2] * slopes[2]
                by_density, by_gradient = potentials(point_density, grad_square)
                densities[t : t + 1, points] = point_density
                scaled = weights[t : t + 1, points] * (1.0 / 4096.0)
                factors = [0.5 * by_density * scaled] + [2.0 * by_gradient * scaled * s for s in slopes]
                z = None
                for k in range(4):
                    factor = jnp.broadcast_to(factors[k], (16, LANES)).astype(jnp.bfloat16)
                    basis = turned[n, k, :, lanes].reshape(FUNCTIONS // 16, 16, LANES)
                    z = factor[None] * basis if z is None else z + factor[None] * basis
                weighted[now, :, lanes] = z.reshape(FUNCTIONS, LANES)

        total[...] += lax.dot_general(
            turned[STEPS * t + STEPS - 1, 0],
            weighted[(STEPS - 1) % 2],
            (((1,), (1,)), ((), ())),
            preferred_element_type=jnp.float32,
        )
        both = total[...] + total[...].T
        for piece in range(12):
            rows_of[piece] = both[SLICE * piece : SLICE * piece + SLICE].astype(jnp.bfloat16)

        @pl.loop(1, COLS + 1)
        def _(step):
            holder = (c + step) % COLS
            for which in range(2):
                piece = holder + 8 * which - shift
                inside = (piece >= 0) & (piece < 12)
                terms[holder, t, which] = rows_of[jnp.where(inside, piece, 12)]

            @pl.when(holder != c)
            def _():
                term_copy(holder, t).start()

            @pl.when(holder == c)
            def _():
                pltpu.make_async_copy(
                    terms.at[holder, t], gathered[t].at[c, pl.ds(0, 2)], recv_terms.at[t]
                ).start()

    def sum_copy(side):
        return pltpu.make_async_remote_copy(
            edges.at[side],
            arrived.at[1 - side],
            send_sum.at[side],
            recv_sum.at[1 - side],
            device_id={"row": q + 2 * side - 1, "col": c},
            device_id_type=pl.DeviceIdType.MESH,
        )

    def add_up(t, lead, which):
        for odd in range(2):
            together = None if t == 0 else sums[lead, which, odd]
            for s in range(COLS):
                start = start_words[s, 0, t]
                chosen = (start // 2 - (4 * q - 1) == lead) & (start % 2 == odd)
                piece = gathered[t][s, jnp.where(chosen, which, 2)].astype(jnp.float32)
                together = piece if together is None else together + piece
            sums[lead, which, odd] = together

    def block_row(r):
        wide = [jnp.zeros((SLICE, HALF), jnp.float32) for _ in range(6)]
        for which in range(2):
            if 0 <= r - which < 5:
                for odd in range(2):
                    piece = sums[r - which, which, odd]
                    for third in range(3):
                        place = 2 + odd - 2 * which + third
                        wide[place] = wide[place] + piece[:, HALF * third : HALF * third + HALF]
        return [jnp.concatenate(wide[2 * d : 2 * d + 2], axis=1) for d in range(3)]

    for t in range(2):
        part = gathered[t].at[:, pl.ds(0, 2)]
        pltpu.make_async_copy(part, part, recv_terms.at[t]).wait()
        add_up(t, 0, 0)
        add_up(t, 4, 1)
        if t == 1:
            for side in range(2):
                for d, block in enumerate(block_row(5 * side)):
                    edges[side, d] = block.astype(jnp.bfloat16)
                reached = (q < 15) if side else (q > 0)

                @pl.when(reached)
                def _():
                    sum_copy(side).start()

        @pl.loop(0, 4)
        def _(lead):
            add_up(t, lead + 1, 0)
            add_up(t, lead, 1)

    for side in range(2):
        reached = (q < 15) if side else (q > 0)

        @pl.when(jnp.logical_not(reached))
        def _():
            arrived[side] = jnp.zeros((3, SLICE, WIDTH), jnp.bfloat16)

    for local in (1, 2, 0, 3):
        if local in (0, 3):
            side = local // 3
            reached = (q < 15) if side else (q > 0)

            @pl.when(reached)
            def _():
                sum_copy(1 - side).wait_recv()

        blocks = block_row(local + 1)
        matrix[local, 0] = jnp.zeros((SLICE, WIDTH), jnp.float32)
        matrix[local, 4] = jnp.zeros((SLICE, WIDTH), jnp.float32)
        for d in range(3):
            block = blocks[d]
            if local in (0, 3):
                block = block + arrived[local // 3, d].astype(jnp.float32)
            matrix[local, d + 1] = jnp.where(pattern[local, d + 1] > 0, block, 0.0)

    for side in range(2):
        reached = (q < 15) if side else (q > 0)

        @pl.when(reached)
        def _():
            sum_copy(side).wait_send()

    @pl.loop(0, 4)
    def _(local):
        first_copies(local, lambda copy, remote: copy.wait_send() if remote else None)

    for role in order:
        k = i + role

        @pl.when((k >= 0) & (k < BLOCKS) & ((k // 4) % 2 == h))
        def _():
            pass_on(role).wait_send()

    own_far.wait_send()
    for role in (-1, 1, -2, 2):
        target = i - role

        @pl.when((target >= 0) & (target < BLOCKS))
        def _():
            second_copy(role).wait_send()

        k = i + role

        @pl.when((k >= 0) & (k < BLOCKS))
        def _():
            second_pass(role).wait_send()

    for part in range(3):
        out_copies(part, lambda copy, remote: copy.wait_send() if remote else None)
    for part, diagonal in ((1, 0), (2, 4)):
        for local in range(4):
            block = purified.at[local, pl.ds(diagonal, 1)]
            pltpu.make_async_copy(block, block, recv_out.at[part, local]).wait()
    edge_copies(lambda copy, remote: copy.wait_send() if remote else None)

    @pl.loop(0, COLS)
    def _(other):
        @pl.when(other != c)
        def _():
            start_copy(other).wait_send()
            for t in range(2):
                window_copy(other, t).wait_send()
                term_copy(other, t).wait_send()


def on_device(density, pattern, windows, basis_values, basis_grads, weights):
    bf16, f32, dma = jnp.bfloat16, jnp.float32, pltpu.SemaphoreType.DMA
    vmem = pl.BlockSpec(memory_space=pltpu.VMEM)
    smem = pl.BlockSpec(memory_space=pltpu.SMEM)
    hbm = pl.BlockSpec(memory_space=pl.ANY)
    half_row = pltpu.VMEM((BAND, HALF, WIDTH), bf16)
    pieces = pltpu.VMEM((COLS, 2, 2, SLICE, FUNCTIONS), bf16)
    edge = pltpu.VMEM((2, 3, SLICE, WIDTH), bf16)
    return pl.pallas_call(
        fused_kernel,
        name="fused",
        in_specs=[vmem, smem, smem, hbm, hbm, vmem],
        out_specs=[vmem, vmem, vmem],
        out_shape=[
            jax.ShapeDtypeStruct(density.shape, bf16),
            jax.ShapeDtypeStruct(density.shape, f32),
            jax.ShapeDtypeStruct(weights.shape, f32),
        ],
        scratch_shapes=[
            pltpu.VMEM(density.shape, bf16),
            pltpu.VMEM((4, 8, WIDTH), f32),
            pltpu.VMEM((4, 8, WIDTH), f32),
            pltpu.VMEM((8, 128), jnp.int32),
            pltpu.VMEM((COLS, 8, 128), jnp.int32),
            pltpu.SMEM((COLS, 8, 128), jnp.int32),
            pltpu.VMEM((2, 4, POINT_BLOCK, FUNCTIONS), bf16),
            pltpu.VMEM((2 * STEPS, 4, FUNCTIONS, POINT_BLOCK), bf16),
            pltpu.VMEM((12, WIDTH, WIDTH), bf16),
            pltpu.VMEM((19, WIDTH, WIDTH), bf16),
            half_row,
            half_row,
            half_row,
            pltpu.VMEM((6, 3, SLICE, WIDTH), bf16),
            pieces,
            pltpu.VMEM((COLS, 2, SLICE, FUNCTIONS), bf16),
            pltpu.VMEM((COLS, 2, SLICE, FUNCTIONS), bf16),
            pltpu.VMEM((FUNCTIONS, FUNCTIONS), bf16),
            pltpu.VMEM((2, FUNCTIONS, POINT_BLOCK), f32),
            pltpu.VMEM((2, FUNCTIONS, POINT_BLOCK), bf16),
            pltpu.VMEM((FUNCTIONS, FUNCTIONS), f32),
            pltpu.VMEM((13, SLICE, FUNCTIONS), bf16),
            pieces,
            pltpu.VMEM((COLS, 3, SLICE, FUNCTIONS), bf16),
            pltpu.VMEM((COLS, 3, SLICE, FUNCTIONS), bf16),
            pltpu.VMEM((5, 2, 2, SLICE, FUNCTIONS), f32),
            edge,
            edge,
            dma((2, 2)),
            dma((2,)),
            dma((COLS,)),
            dma(()),
            dma((4, 6)),
            dma((5,)),
            dma((5,)),
            dma((5,)),
            dma((5,)),
            dma((5,)),
            dma((5,)),
            dma((5,)),
            dma(()),
            dma((3, 4)),
            dma((3, 4)),
            dma((4,)),
            dma((2,)),
            dma((COLS, 2)),
            dma((2,)),
            dma((COLS, 2)),
            dma((2,)),
            dma((2,)),
            dma((2,)),
        ],
        compiler_params=pltpu.CompilerParams(
            collective_id=0, has_side_effects=True, vmem_limit_bytes=63 * 1024 * 1024
        ),
    )(density, pattern, windows, basis_values, basis_grads, weights)


def solution(mesh):
    placed = (
        P("row", None, COL, None),
        P("row", None),
        P(ROW_COL),
        P(ROW_COL, None, None),
        P(None, ROW_COL, None, None),
        P(ROW_COL, None),
    )
    return jax.shard_map(
        on_device,
        mesh=mesh,
        in_specs=placed,
        out_specs=(P("row", None, COL, None), P("row", None, COL, None), P(ROW_COL, None)),
        check_vma=False,
    )
```

time: 120 us -> 92.5 us (0.77)
  Pallas kernels: 109 us -> 86.5 us
  local copies, waits for them, and re-layouts: 8.15 us -> 5.08 us
  other arithmetic: 1.76 us -> 0 us
    pallas_call x3 -> x1, Pallas kernels: 109 us -> 86.5 us  [on_device(): pl.pallas_call(fused_kernel, name='fused', in_specs=[vmem, smem, smem, hb...]
    reshape x3 -> x0, local copies, waits for them, and re-layouts: 2.13 us -> none  [the longest x2 1.22 us: tile_terms(): quadrature.reshape(tiles, steps, 128, 8)]
    unnamed x6 -> x3, local copies, waits for them, and re-layouts: 5 us -> 5.08 us
where the time goes in v4:
time: 92.5 us; the launch traced here: 92.2 us
  Pallas kernels  86.5 us (94%)
  local copies, waits for them, and re-layouts  5.08 us (5%)
    pallas_call x1, Pallas kernels, on_device(): pl.pallas_call(fused_kernel, name='fused', in_specs=[vmem, smem, smem, hb...  86.5 us
    unnamed x3, local copies, waits for them, and re-layouts  5.08 us

profile of v4, /device:TPU:1, one launch (start us, length us, event | category | flops | bytes accessed | tf_op | source)
XLA Modules:
  0.0 92.2 jit_solution(2957419266040190063)
XLA Ops:
  0.6 86.5 %fused.1 = (bf16[4,5,32,256]{3,2,1,0:T(8,128)(2,1)}, f32[4,5,32,256]{3,2,1,0:T(8,128)}, f32[2,4096]{1,0:T(2,128)}) custom-call(bf16[4,5,32,256]{3,2,1,0:T(8,128)(2,1)} %density.1, s32[4,5]{1,0:T(4,128)} %pattern.1, s32[2]{0:T(128)} %windows.1, bf16[2,4096,384]{2,1,0:T(8,128)(2,1)} %values.1, bf16[3,2,4096,384]{3,2,1,0:T(8,128)(2,1)} %grads.1, f32[2,4096]{1,0:T(2,128)} %weights.1), custom_call_target="tpu_custom_call" | custom-call | tf_op jit(solution)/shard_map/fused/pallas_call | solution.py:729
  87.1 1.7 %copy.12 = bf16[4,5,32,256]{3,2,1,0:T(8,128)(2,1)} copy(bf16[4,5,32,256]{3,2,1,0:T(8,128)(2,1)} %get-tuple-element.6) | data formatting | bytes 655360
  88.8 2.0 %copy.13 = f32[4,5,32,256]{3,2,1,0:T(8,128)} copy(f32[4,5,32,256]{3,2,1,0:T(8,128)} %get-tuple-element.7) | data formatting | bytes 1310720
  90.8 1.4 %copy.14 = f32[2,4096]{1,0:T(2,128)} copy(f32[2,4096]{1,0:T(2,128)} %get-tuple-element.8) | data formatting | bytes 65536

commit v5 on v4

--- a/solution.py
+++ b/solution.py
@@ -37,6 +37,7 @@
 HALF = 128
 WIDTH = 256
 SLICE = 32
+PART = 16
 COLS = 8
 FIRST_PIECES = {
     -2: ((2, 2, 0),),
@@ -134,8 +135,8 @@
     own_sem,
     send_out,
     recv_out,
-    send_edge,
-    recv_edge,
+    send_near,
+    recv_near,
     send_window,
     recv_window,
     send_terms,
@@ -194,20 +195,18 @@
         def _():
             greet(q + 2, other)
 
-        @pl.when((m > 0) & (h == 0) & (((c == 0) & (other <= 3)) | ((c >= 4) & (other == 7)) | (other == c)))
+        @pl.when((m > 0) & (h == 0) & ((c == 0) | (other == 7) | (other == c)))
         def _():
             greet(q - 1, other)
 
-        @pl.when((m < 7) & (h == 1) & (((c == 7) & (other >= 4)) | ((c <= 3) & (other == 0)) | (other == c)))
+        @pl.when((m < 7) & (h == 1) & ((c == 7) | (other == 0) | (other == c)))
         def _():
             greet(q + 1, other)
 
     lower = jnp.where(m > 0, jnp.where(h == 0, 2, jnp.where(c % 4 == 0, 8, 0)), 0)
     upper = jnp.where(m < 7, jnp.where(h == 1, 2, jnp.where(c % 4 == 3, 8, 0)), 0)
-    some = jnp.where((c >= 4) & (c <= 6), 2, 1)
-    lower_side = jnp.where((m > 0) & (h == 0), jnp.where(c == 0, 4, some), 0)
-    some = jnp.where((c >= 1) & (c <= 3), 2, 1)
-    upper_side = jnp.where((m < 7) & (h == 1), jnp.where(c == 7, 4, some), 0)
+    lower_side = jnp.where((m > 0) & (h == 0), jnp.where(c == 0, 8, jnp.where(c == 7, 1, 2)), 0)
+    upper_side = jnp.where((m < 7) & (h == 1), jnp.where(c == 7, 8, jnp.where(c == 0, 1, 2)), 0)
 
     for local in range(4):
         for d in range(BAND):
@@ -384,11 +383,10 @@
     own_far.wait_recv()
     iterate(lambda a: mine[a], second, second_block, final)
 
-    def out_copies(part, act):
-        diagonal, count = ((1, 3), (0, 1), (4, 1))[part]
+    def out_copies(act):
         for u in range(4):
-            source = final.at[pl.ds(diagonal, count), pl.ds(SLICE * u, SLICE)]
-            landing = purified.at[j % 4, pl.ds(diagonal, count)]
+            source = final.at[:, pl.ds(SLICE * u, SLICE)]
+            landing = purified.at[j % 4]
             row, col = 2 * m + j // 4, 4 * h + u
             here = (row == q) & (col == c)
 
@@ -398,8 +396,8 @@
                     pltpu.make_async_remote_copy(
                         source,
                         landing,
-                        send_out.at[part, u],
-                        recv_out.at[part, j % 4],
+                        send_out.at[u],
+                        recv_out.at[j % 4],
                         device_id={"row": row, "col": col},
                         device_id_type=pl.DeviceIdType.MESH,
                     ),
@@ -408,19 +406,25 @@
 
             @pl.when(here)
             def _():
-                act(pltpu.make_async_copy(source, landing, recv_out.at[part, j % 4]), False)
-
-    def edge_copies(act):
-        for side, reach, slot in ((0, -1, 5), (3, 1, 0)):
-            row = 2 * m + j // 4 + reach
-
-            @pl.when((j % 4 == side) & (row >= 0) & (row < 16))
+                act(pltpu.make_async_copy(source, landing, recv_out.at[j % 4]), False)
+
+    def near_copies(act):
+        home = 2 * m + j // 4
+        for lane_of, (row, slot, group, needed) in enumerate(
+            (
+                (home, 2 * (j % 4 + 1) + h, 0, home >= 0),
+                (home - 1, 10 + h, 2, (j % 4 == 0) & (home > 0)),
+                (home + 1, h, 1, (j % 4 == 3) & (home < 15)),
+            )
+        ):
+
+            @pl.when(needed)
             def _():
-                for u in range(4):
-                    here = (row == q) & (4 * h + u == c)
-                    source = final.at[pl.ds(1, 3), pl.ds(SLICE * u, SLICE)]
+                @pl.loop(0, COLS)
+                def _(u):
+                    here = (row == q) & (u == c)
+                    source = final.at[pl.ds(1, 3), pl.ds(pl.multiple_of(PART * u, PART), PART)]
                     landing = near.at[slot]
-                    arrived = recv_edge.at[slot // 5]
 
                     @pl.when(jnp.logical_not(here))
                     def _():
@@ -428,9 +432,9 @@
                             pltpu.make_async_remote_copy(
                                 source,
                                 landing,
-                                send_edge.at[u],
-                                arrived,
-                                device_id={"row": row, "col": 4 * h + u},
+                                send_near.at[lane_of, u],
+                                recv_near.at[group],
+                                device_id={"row": row, "col": u},
                                 device_id_type=pl.DeviceIdType.MESH,
                             ),
                             True,
@@ -438,30 +442,23 @@
 
                     @pl.when(here)
                     def _():
-                        act(pltpu.make_async_copy(source, landing, arrived), False)
-
-    edge_copies(lambda copy, remote: copy.start())
-    out_copies(0, lambda copy, remote: copy.start())
+                        act(pltpu.make_async_copy(source, landing, recv_near.at[group]), False)
+
+    near_copies(lambda copy, remote: copy.start())
     pltpu.make_async_copy(all_starts, all_starts, recv_starts).wait()
     words = pltpu.make_async_copy(all_starts, start_words, own_sem)
     words.start()
     words.wait()
-    for local in range(4):
-        part = purified.at[local, pl.ds(1, 3)]
-        pltpu.make_async_copy(part, part, recv_out.at[0, local]).wait()
-        near[local + 1] = purified[local, pl.ds(1, 3)]
-
-    for side in range(2):
-        part = near.at[5 * side]
-        reached = (q < 15) if side else (q > 0)
+    for group, first_slot, count, reached in ((0, 2, 8, q >= 0), (1, 0, 2, q > 0), (2, 10, 2, q < 15)):
+        part = near.at[pl.ds(first_slot, count)]
 
         @pl.when(reached)
         def _():
-            pltpu.make_async_copy(part, part, recv_edge.at[side]).wait()
+            pltpu.make_async_copy(part, part, recv_near.at[group]).wait()
 
         @pl.when(jnp.logical_not(reached))
         def _():
-            near[5 * side] = jnp.zeros((3, SLICE, WIDTH), jnp.bfloat16)
+            near[pl.ds(first_slot, count)] = jnp.zeros((count, 3, PART, WIDTH), jnp.bfloat16)
 
     def window_copy(other, t):
         return pltpu.make_async_remote_copy(
@@ -479,17 +476,18 @@
         def _(step):
             other = (c + step) % COLS
             start = start_words[other, 0, t]
-            lead = jnp.clip(start // 2 - (4 * q - 1), 0, 4)
+            lead = jnp.clip(start - 2 * (4 * q - 1), 0, 9)
             odd = (start % 2) == 1
-            for which in range(2):
-                left = near[lead + which, 1 - which]
-                right = near[lead + which, 2 - which]
+            for third_row in range(3):
+                at = (1, jnp.where(odd, 0, 1), 0)[third_row]
+                left = near[lead + third_row, at]
+                right = near[lead + third_row, at + 1]
                 for third, even_part, odd_part in (
                     (0, left[:, :128], left[:, 128:]),
                     (1, left[:, 128:], right[:, :128]),
                     (2, right[:, :128], right[:, 128:]),
                 ):
-                    ready[other, t, which, :, 128 * third : 128 * third + 128] = jnp.where(
+                    ready[other, t, third_row, :, 128 * third : 128 * third + 128] = jnp.where(
                         odd, odd_part, even_part
                     )
 
@@ -501,8 +499,7 @@
             def _():
                 pltpu.make_async_copy(ready.at[other, t], staged[t].at[c], recv_window.at[t]).start()
 
-    for part in (1, 2):
-        out_copies(part, lambda copy, remote: copy.start())
+    out_copies(lambda copy, remote: copy.start())
 
     def term_copy(other, t):
         return pltpu.make_async_remote_copy(
@@ -524,9 +521,10 @@
         part = staged[t]
         pltpu.make_async_copy(part, part, recv_window.at[t]).wait()
         shift = 4 * (start_words[c, 0, t] % 2)
-        for u in range(12):
-            at = shift + u
-            window[SLICE * u : SLICE * u + SLICE, :] = staged[t][at % 8, at // 8]
+        for third_row in range(3):
+            for u in range(COLS):
+                place = HALF * third_row + PART * u
+                window[place : place + PART, :] = staged[t][u, third_row]
         window[...] = window[...].T
         total[...] = jnp.zeros_like(total)
         weighted[1] = jnp.zeros((FUNCTIONS, POINT_BLOCK), jnp.bfloat16)
@@ -700,13 +698,11 @@
         def _():
             second_pass(role).wait_send()
 
-    for part in range(3):
-        out_copies(part, lambda copy, remote: copy.wait_send() if remote else None)
-    for part, diagonal in ((1, 0), (2, 4)):
-        for local in range(4):
-            block = purified.at[local, pl.ds(diagonal, 1)]
-            pltpu.make_async_copy(block, block, recv_out.at[part, local]).wait()
-    edge_copies(lambda copy, remote: copy.wait_send() if remote else None)
+    out_copies(lambda copy, remote: copy.wait_send() if remote else None)
+    near_copies(lambda copy, remote: copy.wait_send() if remote else None)
+    for local in range(4):
+        block = purified.at[local]
+        pltpu.make_async_copy(block, block, recv_out.at[local]).wait()
 
     @pl.loop(0, COLS)
     def _(other):
@@ -716,6 +712,11 @@
             for t in range(2):
                 window_copy(other, t).wait_send()
                 term_copy(other, t).wait_send()
+
+
+def hand_over(*refs):
+    for source, target in zip(refs[:3], refs[3:]):
+        target[...] = source[...]
 
 
 def on_device(density, pattern, windows, basis_values, basis_grads, weights):
@@ -726,7 +727,7 @@
     half_row = pltpu.VMEM((BAND, HALF, WIDTH), bf16)
     pieces = pltpu.VMEM((COLS, 2, 2, SLICE, FUNCTIONS), bf16)
     edge = pltpu.VMEM((2, 3, SLICE, WIDTH), bf16)
-    return pl.pallas_call(
+    results = pl.pallas_call(
         fused_kernel,
         name="fused",
         in_specs=[vmem, smem, smem, hbm, hbm, vmem],
@@ -750,10 +751,10 @@
             half_row,
             half_row,
             half_row,
-            pltpu.VMEM((6, 3, SLICE, WIDTH), bf16),
-            pieces,
-            pltpu.VMEM((COLS, 2, SLICE, FUNCTIONS), bf16),
-            pltpu.VMEM((COLS, 2, SLICE, FUNCTIONS), bf16),
+            pltpu.VMEM((12, 3, PART, WIDTH), bf16),
+            pltpu.VMEM((COLS, 2, 3, PART, FUNCTIONS), bf16),
+            pltpu.VMEM((COLS, 3, PART, FUNCTIONS), bf16),
+            pltpu.VMEM((COLS, 3, PART, FUNCTIONS), bf16),
             pltpu.VMEM((FUNCTIONS, FUNCTIONS), bf16),
             pltpu.VMEM((2, FUNCTIONS, POINT_BLOCK), f32),
             pltpu.VMEM((2, FUNCTIONS, POINT_BLOCK), bf16),
@@ -778,10 +779,10 @@
             dma((5,)),
             dma((5,)),
             dma(()),
-            dma((3, 4)),
-            dma((3, 4)),
             dma((4,)),
-            dma((2,)),
+            dma((4,)),
+            dma((3, COLS)),
+            dma((3,)),
             dma((COLS, 2)),
             dma((2,)),
             dma((COLS, 2)),
@@ -793,6 +794,13 @@
             collective_id=0, has_side_effects=True, vmem_limit_bytes=63 * 1024 * 1024
         ),
     )(density, pattern, windows, basis_values, basis_grads, weights)
+    return pl.pallas_call(
+        hand_over,
+        name="hand_over",
+        in_specs=[vmem, vmem, vmem],
+        out_specs=[vmem, vmem, vmem],
+        out_shape=[jax.ShapeDtypeStruct(r.shape, r.dtype) for r in results],
+    )(*results)
 
 
 def solution(mesh):

time: 92.5 us -> 89 us (0.962)
  local copies, waits for them, and re-layouts: 5.08 us -> 0 us
  Pallas kernels: 86.5 us -> 88.1 us
    unnamed x3 -> x0, local copies, waits for them, and re-layouts: 5.08 us -> none
    pallas_call x0 -> x1, Pallas kernels: none -> 2.16 us  [on_device(): pl.pallas_call(hand_over, name='hand_over', in_specs=[vmem, vmem, vmem],...]
where the time goes in v5:
time: 89 us; the launch traced here: 88.8 us
  Pallas kernels  88.1 us (99%)
    pallas_call x1, Pallas kernels, on_device(): pl.pallas_call(fused_kernel, name='fused', in_specs=[vmem, smem, smem, hb...  86 us
    pallas_call x1, Pallas kernels, on_device(): pl.pallas_call(hand_over, name='hand_over', in_specs=[vmem, vmem, vmem],...  2.16 us

profile of v5, /device:TPU:1, one launch (start us, length us, event | category | flops | bytes accessed | tf_op | source)
XLA Modules:
  0.0 88.8 jit_solution(2944276587616251338)
XLA Ops:
  0.6 86.0 %fused.1 = (bf16[4,5,32,256]{3,2,1,0:T(8,128)(2,1)}, f32[4,5,32,256]{3,2,1,0:T(8,128)}, f32[2,4096]{1,0:T(2,128)}) custom-call(bf16[4,5,32,256]{3,2,1,0:T(8,128)(2,1)} %density.1, s32[4,5]{1,0:T(4,128)} %pattern.1, s32[2]{0:T(128)} %windows.1, bf16[2,4096,384]{2,1,0:T(8,128)(2,1)} %values.1, bf16[3,2,4096,384]{3,2,1,0:T(8,128)(2,1)} %grads.1, f32[2,4096]{1,0:T(2,128)} %weights.1), custom_call_target="tpu_custom_call" | custom-call | tf_op jit(solution)/shard_map/fused/pallas_call | solution.py:730
  86.6 2.2 %hand_over.1 = (bf16[4,5,32,256]{3,2,1,0:T(8,128)(2,1)}, f32[4,5,32,256]{3,2,1,0:T(8,128)}, f32[2,4096]{1,0:T(2,128)}) custom-call(bf16[4,5,32,256]{3,2,1,0:T(8,128)(2,1)} %get-tuple-element.6.refs_0_, f32[4,5,32,256]{3,2,1,0:T(8,128)} %get-tuple-element.7.refs_1_, f32[2,4096]{1,0:T(2,128)} %get-tuple-element.8.refs_2_), custom_call_target="tpu_custom_call" | custom-call | tf_op jit(solution)/shard_map/hand_over/pallas_call | solution.py:797

commit v6 on v5

--- a/solution.py
+++ b/solution.py
@@ -600,12 +600,13 @@
             device_id_type=pl.DeviceIdType.MESH,
         )
 
+    lowest = 2 * (4 * q - 1)
+
     def add_up(t, lead, which):
         for odd in range(2):
             together = None if t == 0 else sums[lead, which, odd]
             for s in range(COLS):
-                start = start_words[s, 0, t]
-                chosen = (start // 2 - (4 * q - 1) == lead) & (start % 2 == odd)
+                chosen = start_words[s, 0, t] == lowest + 2 * lead + odd
                 piece = gathered[t][s, jnp.where(chosen, which, 2)].astype(jnp.float32)
                 together = piece if together is None else together + piece
             sums[lead, which, odd] = together

time: 89 us -> 88.9 us (level)
  no operation moved by 1% of the time
where the time goes in v6:
time: 88.9 us; the launch traced here: 88.7 us
  Pallas kernels  88.1 us (99%)
    pallas_call x1, Pallas kernels, on_device(): pl.pallas_call(fused_kernel, name='fused', in_specs=[vmem, smem, smem, hb...  85.9 us
    pallas_call x1, Pallas kernels, on_device(): pl.pallas_call(hand_over, name='hand_over', in_specs=[vmem, vmem, vmem],...  2.16 us

profile of v6, /device:TPU:1, one launch (start us, length us, event | category | flops | bytes accessed | tf_op | source)
XLA Modules:
  0.0 88.7 jit_solution(1399645731284785605)
XLA Ops:
  0.6 85.9 %fused.1 = (bf16[4,5,32,256]{3,2,1,0:T(8,128)(2,1)}, f32[4,5,32,256]{3,2,1,0:T(8,128)}, f32[2,4096]{1,0:T(2,128)}) custom-call(bf16[4,5,32,256]{3,2,1,0:T(8,128)(2,1)} %density.1, s32[4,5]{1,0:T(4,128)} %pattern.1, s32[2]{0:T(128)} %windows.1, bf16[2,4096,384]{2,1,0:T(8,128)(2,1)} %values.1, bf16[3,2,4096,384]{3,2,1,0:T(8,128)(2,1)} %grads.1, f32[2,4096]{1,0:T(2,128)} %weights.1), custom_call_target="tpu_custom_call" | custom-call | tf_op jit(solution)/shard_map/fused/pallas_call | solution.py:731
  86.6 2.2 %hand_over.1 = (bf16[4,5,32,256]{3,2,1,0:T(8,128)(2,1)}, f32[4,5,32,256]{3,2,1,0:T(8,128)}, f32[2,4096]{1,0:T(2,128)}) custom-call(bf16[4,5,32,256]{3,2,1,0:T(8,128)(2,1)} %get-tuple-element.6.refs_0_, f32[4,5,32,256]{3,2,1,0:T(8,128)} %get-tuple-element.7.refs_1_, f32[2,4096]{1,0:T(2,128)} %get-tuple-element.8.refs_2_), custom_call_target="tpu_custom_call" | custom-call | tf_op jit(solution)/shard_map/hand_over/pallas_call | solution.py:798
